TPU v7x, 32 devices: a whole 2x2x4 slice. The times are simulated.
32 devices in a mesh: ent: 2 (over x), blk: 4 (over y, core), rel: 4 (over z).
Axes of the slice: x: 2, y: 2, z: 4, core: 2. Of those that a mesh axis runs over, the one named last changes fastest.
Arguments:
- factors: bfloat16 [8192, 256], P(('ent', 'blk')), may hold values from -12 to 12
- heads: int32 [8, 4, 1, 8192], P(None, 'rel', None, ('ent', 'blk')), may hold values from 0 to 1023, as said below
- tails: int32 [8, 4, 1, 8192], P(None, 'rel', None, ('ent', 'blk')), may hold values from 0 to 1023, as said below
- values: float32 [8, 4, 1, 8192], P(None, 'rel', None, ('ent', 'blk')), may hold values from 0.3 to 9
Outputs:
- relation_fit: float32 [32, 256, 256], P(('ent', 'blk', 'rel'))
- residual: float32 [32, 256, 256], P(('ent', 'blk', 'rel'))
Inputs may be any that keep to these rules, and one draw needn't show every extreme that they name: In every aligned tile of 128 triple columns (columns 128 t to 128 t + 127 of one relation) all heads lie in one aligned block of 128 positions (128 b to 128 b + 127). In every aligned tile of 128 triple columns all tails lie in one aligned block of 128 positions.
All inputs are finite; a program needn't handle non-finite values.
Results may differ from a plain program's by a relative error of at most 0.0029.
Values sent between devices are 32-bit elements; how exact they have to be, the bound alone decides.
A program may use at most 128 MiB of HBM per device.

v0:
```python
import functools
import math

import jax
import jax.numpy as jnp
from jax import lax
from jax.experimental import pallas as pl
from jax.experimental.pallas import tpu as pltpu
from jax.sharding import PartitionSpec as P

ITERS = 8


ridge_weight = 0.01
tile_width = 128


def apply_normal(gram_matrix, stacked):
    left_side = jnp.einsum("ab,kbc->kac", gram_matrix, stacked, precision=lax.Precision.HIGHEST)
    return (
        jnp.einsum("kac,cd->kad", left_side, gram_matrix, precision=lax.Precision.HIGHEST)
        + ridge_weight * stacked
    )


def two_products(residual, image_map):
    return lax.psum(
        (jnp.sum(residual * residual), jnp.sum(residual * image_map)), ("ent", "blk", "rel")
    )


def select_rows(entity_ids, block_table):
    group_size, width = entity_ids.shape
    tile_count = width // tile_width
    block_count = block_table.shape[0]
    tiled_ids = entity_ids.reshape(group_size, tile_count, tile_width)
    block_of = tiled_ids[:, :, 0] // tile_width
    block_pick = (
        block_of[:, :, None] == jnp.arange(block_count, dtype=jnp.int32)[None, None, :]
    ).astype(jnp.bfloat16)
    chosen = jnp.einsum(
        "gtb,bcr->gtcr", block_pick, block_table, preferred_element_type=jnp.float32
    ).astype(jnp.bfloat16)
    inside = tiled_ids % tile_width
    slot_pick = (
        inside[:, :, :, None] == jnp.arange(tile_width, dtype=jnp.int32)[None, None, None, :]
    ).astype(jnp.bfloat16)
    return jnp.einsum("gtoc,gtcr->gtor", slot_pick, chosen, preferred_element_type=jnp.float32)


def body(factors, heads, tails, values):
    shards = lax.axis_size(("ent", "blk"))
    ent_dev = factors.shape[0]
    rank_width = factors.shape[1]
    triple_count = heads.shape[3]
    relation_rows = heads.shape[0] * heads.shape[2]
    norm_scale = 1.0 / math.sqrt(shards * triple_count)
    gram_total = lax.psum(
        jnp.dot(factors.T, factors, preferred_element_type=jnp.float32), ("ent", "blk")
    )
    gram_matrix = gram_total / (ent_dev * shards)
    block_table = factors.reshape(ent_dev // tile_width, tile_width, rank_width)
    head_ids = heads.reshape(relation_rows, triple_count)
    tail_ids = tails.reshape(relation_rows, triple_count)
    weights = values.reshape(relation_rows, triple_count)

    def grouped(operands):
        head_group, tail_group, weight_group = operands
        group_size = head_group.shape[0]
        tile_count = triple_count // tile_width
        head_rows = select_rows(head_group, block_table)
        weighted = (
            weight_group.reshape(group_size, tile_count, tile_width)[:, :, :, None] * head_rows
        ).astype(jnp.bfloat16)
        tail_rows = select_rows(tail_group, block_table).astype(jnp.bfloat16)
        product = jnp.einsum(
            "gtci,gtcj->gij", weighted, tail_rows, preferred_element_type=jnp.float32
        )
        return product * norm_scale

    own_rows = relation_rows // shards
    group_size = math.gcd(own_rows * lax.axis_size(("ent", "blk")), 4)
    group_total = own_rows * lax.axis_size(("ent", "blk")) // group_size
    shaped = (
        head_ids.reshape(group_total, group_size, triple_count),
        tail_ids.reshape(group_total, group_size, triple_count),
        weights.reshape(group_total, group_size, triple_count),
    )
    results = lax.map(grouped, shaped)
    target = lax.psum_scatter(
        results.reshape(own_rows * lax.axis_size(("ent", "blk")), rank_width, rank_width),
        ("ent", "blk"),
        scatter_dimension=0,
        tiled=True,
    )
    fitted = jnp.zeros_like(target)
    residual = target
    image_map = apply_normal(gram_matrix, residual)
    norm_now, product = two_products(residual, image_map)
    step_size = norm_now / product
    direction = residual
    along = image_map
    for step_index in range(ITERS):
        fitted = fitted + step_size * direction
        residual = residual - step_size * along
        if step_index + 1 < ITERS:
            image_map = apply_normal(gram_matrix, residual)
            norm_next, product = two_products(residual, image_map)
            ratio_next = norm_next / norm_now
            step_size = norm_next / (product - ratio_next * norm_next / step_size)
            direction = residual + ratio_next * direction
            along = image_map + ratio_next * along
            norm_now = norm_next
    return (fitted, residual)


MESH = pl.DeviceIdType.MESH
COPIES = 64


def fused_kernel(
    z_count, scale_gram, scale_target,
    factors_hbm, heads_hbm, tails_hbm, values_hbm,
    fit_ref, res_ref,
    factors_ref, heads_ref, tails_ref, values_ref, head_ids, tail_ids, load_sem, ready,
    turned, left_rows, right_rows,
    gram_part, gram_in, gram_half, gram_xy, gram_line, gram_full, gram_pair,
    pair_out, pair_in, own_sum, first_a, first_b, second_a, second_b,
    basis, table, send_sem, recv_sem,
):
    f32, bf16 = jnp.float32, jnp.bfloat16
    width = factors_ref.shape[1]
    half = width // 2
    share = half // z_count
    part = share // 2
    triples = heads_ref.shape[3]
    e = lax.axis_index("ent")
    b = lax.axis_index("blk")
    z = lax.axis_index("rel")
    y = b // 2
    c = b % 2
    pair_peer = (e, y * 2 + 1 - c, z)
    x_peer = (1 - e, b, z)
    y_peer = (e, (1 - y) * 2 + c, z)

    def group_peer(mask):
        me, my, mc = mask // 4, (mask // 2) % 2, mask % 2
        return (
            (1 - e) if me else e,
            ((1 - y) if my else y) * 2 + ((1 - c) if mc else c),
            z,
        )

    def z_peer(hop):
        return (e, b, lax.rem(z + hop, z_count))

    near = [group_peer(m) for m in (1, 2, 4)]
    inner = ((z > 0, -1), (z < z_count - 1, 1))

    def tell(semaphore):
        for present, hop in inner:
            @pl.when(present)
            def _():
                pl.semaphore_signal(
                    semaphore, inc=1, device_id=(e, b, z + hop), device_id_type=MESH
                )

    line_count = jnp.where(z > 0, 1, 0) + jnp.where(z < z_count - 1, 1, 0)
    barrier = pltpu.get_barrier_semaphore()
    for peer in near:
        pl.semaphore_signal(barrier, inc=1, device_id=peer, device_id_type=MESH)
    tell(barrier)
    loads = []
    for slot, (source, dest) in enumerate(
        (
            (factors_hbm, factors_ref),
            (heads_hbm, head_ids),
            (tails_hbm, tail_ids),
            (heads_hbm, heads_ref),
            (values_hbm, values_ref),
            (tails_hbm, tails_ref),
        )
    ):
        loads.append(pltpu.make_async_copy(source, dest, load_sem.at[slot]))
        loads[-1].start()

    counter = [0]

    def send(source, dest, peer):
        slot = counter[0]
        counter[0] += 1
        copy = pltpu.make_async_remote_copy(
            src_ref=source, dst_ref=dest,
            send_sem=send_sem.at[slot], recv_sem=recv_sem.at[slot],
            device_id=peer, device_id_type=MESH,
        )
        copy.start()
        return copy

    loads[0].wait()
    flipped = factors_ref[...].T
    for block in range(turned.shape[0]):
        turned[block] = flipped[:, block * tile_width : (block + 1) * tile_width]
    gram_part[...] = lax.dot_general(
        flipped, flipped, (((1,), (1,)), ((), ())), preferred_element_type=f32
    )
    own_rows = pl.ds(pl.multiple_of(c * half, half), half)
    other_rows = pl.ds(pl.multiple_of((1 - c) * half, half), half)
    own_share = pl.ds(pl.multiple_of(c * half + z * share, share), share)
    other_share = pl.ds(pl.multiple_of((1 - c) * half + z * share, share), share)

    row_number = lax.broadcasted_iota(jnp.int32, (tile_width, tile_width), 0)
    blank = jnp.zeros((tile_width, tile_width), bf16)

    def gathered(ids_ref, scalar_ref, q, first):
        picks, blocks = [], []
        for tile in (first, first + 1):
            start = tile * tile_width
            inside = lax.rem(ids_ref[q, 0, :, start : start + tile_width], tile_width)
            picks.append(jnp.where(row_number == inside, 1.0, 0.0).astype(bf16))
            blocks.append(turned[lax.div(scalar_ref[q, 0, 0, start], tile_width)])
        mixed = jnp.concatenate(
            [
                jnp.concatenate([picks[0], blank], axis=1),
                jnp.concatenate([blank, picks[1]], axis=1),
            ],
            axis=0,
        )
        return jnp.dot(jnp.concatenate(blocks, axis=1), mixed, preferred_element_type=f32)

    def partial(pe, py, pc):
        q = pe * 4 + py * 2 + pc
        for first in range(0, triples // tile_width, 2):
            cols = slice(first * tile_width, (first + 2) * tile_width)
            rows = gathered(heads_ref, head_ids, q, first)
            left_rows[:, cols] = (values_ref[q, 0, :, cols] * rows).astype(bf16)
            right_rows[:, cols] = gathered(tails_ref, tail_ids, q, first).astype(bf16)
        return lax.dot_general(
            left_rows[...], right_rows[...], (((1,), (1,)), ((), ())), preferred_element_type=f32
        )

    targets = ((1 - e, 1 - y), (1 - e, y), (e, 1 - y), (e, y))
    pair_copies = []

    def give(index):
        pe, py = targets[index]
        pair_out[index] = partial(pe, py, 1 - c)
        pair_copies.append(send(pair_out.at[index], pair_in.at[index], pair_peer))

    def keep(index):
        pe, py = targets[index]
        own_sum[index] = partial(pe, py, c)
        pair_copies[index].wait()
        own_sum[index] = own_sum[index] + pair_in[index]

    top, low = pl.ds(0, half), pl.ds(half, half)
    for load in loads[1:]:
        load.wait()
    pair_out[0] = partial(1 - e, 1 - y, 1 - c)
    pl.semaphore_wait(barrier, len(near) + line_count)
    g_pair = send(gram_part.at[other_share], gram_in, pair_peer)
    pair_copies.append(send(pair_out.at[0], pair_in.at[0], pair_peer))
    for step in range(z_count - 2):
        tell(ready.at[step])
        if step + 1 < z_count - 2:
            pl.semaphore_wait(ready.at[step], line_count)
    g_pair.wait()
    gram_half[0] = gram_part[own_share, :] + gram_in[...]
    upper, lower = pl.ds(0, part), pl.ds(part, part)
    g_a1 = send(gram_half.at[0, upper], gram_xy.at[0, upper], x_peer)
    g_b1 = send(gram_half.at[0, lower], gram_xy.at[0, lower], y_peer)
    keep(0)
    a_diag = send(own_sum.at[0, top], first_a.at[0], x_peer)
    b_diag = send(own_sum.at[0, low], first_b.at[0], y_peer)
    give(1)
    g_a1.wait()
    g_b1.wait()
    gram_half[1] = gram_half[0] + gram_xy[0]
    g_a2 = send(gram_half.at[1, upper], gram_xy.at[1, upper], y_peer)
    g_b2 = send(gram_half.at[1, lower], gram_xy.at[1, lower], x_peer)
    keep(1)
    a_side = send(own_sum.at[1, top], first_a.at[1], x_peer)
    give(2)
    g_a2.wait()
    g_b2.wait()
    gram_line[0] = gram_half[1] + gram_xy[1]
    if z_count > 2:
        pl.semaphore_wait(ready.at[z_count - 3], line_count)
    line_copies = [
        send(gram_line.at[0], gram_line.at[z_count - hop], z_peer(hop))
        for hop in range(1, z_count)
    ]
    keep(2)
    b_side = send(own_sum.at[2, low], first_b.at[1], y_peer)
    a_diag.wait()
    second_a[0] = own_sum[2, :half, :] + first_a[0]
    a_last = send(second_a.at[0], second_a.at[1], y_peer)
    b_diag.wait()
    second_b[0] = own_sum[1, half:, :] + first_b[0]
    b_last = send(second_b.at[0], second_b.at[1], x_peer)
    give(3)
    keep(3)
    for copy in line_copies:
        copy.wait()
    for hop in range(z_count):
        place = lax.rem(z + hop, z_count)
        gram_pair[0, pl.ds(pl.multiple_of(place * share, share), share), :] = gram_line[hop]
    g_full = send(gram_pair.at[0], gram_pair.at[1], pair_peer)
    g_full.wait()
    gram_full[own_rows, :] = gram_pair[0] * scale_gram
    gram_full[other_rows, :] = gram_pair[1] * scale_gram
    gram = gram_full[...]
    gram_high = gram.astype(bf16)
    gram_low = (gram - gram_high.astype(f32)).astype(bf16)
    gram_both = jnp.concatenate([gram_high, gram_low], axis=0)
    a_side.wait()
    b_side.wait()
    a_last.wait()
    b_last.wait()
    basis[0, :half, :] = ((own_sum[3, :half, :] + first_a[1]) + second_a[1]) * scale_target
    basis[0, half:, :] = ((own_sum[3, half:, :] + first_b[1]) + second_b[1]) * scale_target

    def split(value):
        high = value.astype(bf16)
        return high, (value - high.astype(f32)).astype(bf16)

    def total(value):
        return jnp.sum(jnp.sum(value, axis=0, keepdims=True), axis=1, keepdims=True)

    def normal_map(value):
        high, low_part = split(value)
        both = jnp.dot(gram_both, high, preferred_element_type=f32)
        inner = both[:width] + (
            both[width:] + jnp.dot(gram_high, low_part, preferred_element_type=f32)
        )
        high, low_part = split(inner)
        both = jnp.dot(
            jnp.concatenate([high, low_part], axis=0), gram_high, preferred_element_type=f32
        )
        outer = both[:width] + (
            both[width:] + jnp.dot(high, gram_low, preferred_element_type=f32)
        )
        return outer + ridge_weight * value

    lane = lax.broadcasted_iota(jnp.int32, (1, 128), 1)
    record = jnp.zeros((1, 128), f32)
    inverses = []
    for index in range(ITERS):
        vector = basis[index]
        image = normal_map(vector)
        square = total(vector * vector)
        cross = total(vector * image)
        inverse = jnp.where(square > 0.0, lax.rsqrt(square), 0.0)
        length = square * inverse
        diagonal = (cross * inverse) * inverse
        record = jnp.where(lane == index, diagonal, record)
        record = jnp.where(lane == ITERS + index, length, record)
        if index + 1 == ITERS:
            table[0, 0] = record
            far_copies = [
                send(
                    table.at[0, 0],
                    table.at[m, (z_count - hop) % z_count],
                    group_peer(m)[:2] + (lax.rem(z + hop, z_count),),
                )
                for hop in range(z_count)
                for m in range(8)
                if m or hop
            ]
        following = (image - diagonal * vector) * inverse
        if index > 0:
            following = following - (length * inverses[-1]) * basis[index - 1]
        inverses.append(inverse)
        basis[index + 1] = following
    for copy in far_copies:
        copy.wait()

    lines = table[...].reshape(8 * z_count, 128)
    filled = jnp.concatenate([lines, jnp.zeros((128 - 8 * z_count, 128), f32)], axis=0).T
    alpha = [filled[j : j + 1, :] for j in range(ITERS)]
    beta = [filled[ITERS + j : ITERS + j + 1, :] for j in range(ITERS)] + [
        jnp.ones((1, 128), f32)
    ]

    def reduced(rows):
        added = rows[0]
        for row in rows[1:]:
            added = added + row
        return jnp.sum(added, axis=1, keepdims=True)

    def small_map(rows):
        count = len(rows)
        made = []
        for j in range(count + 1):
            entry = None
            if j < count:
                entry = alpha[j] * rows[j]
            if j > 0:
                term = beta[j] * rows[j - 1]
                entry = term if entry is None else entry + term
            if j + 1 < count:
                entry = entry + beta[j + 1] * rows[j + 1]
            made.append(entry)
        return made

    def mixed_sum(first, ratio, second):
        return [
            one + ratio * second[j] if j < len(second) else one for j, one in enumerate(first)
        ]

    residual = [beta[0]]
    image = small_map(residual)
    norm_now = reduced([row * row for row in residual])
    product = reduced([row * image[j] for j, row in enumerate(residual)])
    step_size = norm_now / product
    direction, along = residual, image
    fitted = []
    for index in range(ITERS):
        fitted = [
            fitted[j] + step_size * row if j < len(fitted) else step_size * row
            for j, row in enumerate(direction)
        ]
        residual = [
            residual[j] - step_size * row if j < len(residual) else -(step_size * row)
            for j, row in enumerate(along)
        ]
        if index + 1 < ITERS:
            image = small_map(residual)
            norm_next = reduced([row * row for row in residual])
            product = reduced([row * image[j] for j, row in enumerate(residual)])
            ratio = norm_next / norm_now
            step_size = norm_next / (product - ratio * norm_next / step_size)
            direction = mixed_sum(residual, ratio, direction)
            along = mixed_sum(image, ratio, along)
            norm_now = norm_next
    inverses.append(jnp.ones((1, 1), f32))
    fit_weights = [row[:, 0:1] * inverses[j] for j, row in enumerate(fitted)]
    res_weights = [row[:, 0:1] * inverses[j] for j, row in enumerate(residual)]
    fit = fit_weights[0] * basis[0]
    res = res_weights[0] * basis[0]
    for j in range(1, ITERS):
        fit = fit + fit_weights[j] * basis[j]
        res = res + res_weights[j] * basis[j]
    fit_ref[0] = fit
    res_ref[0] = res + res_weights[ITERS] * basis[ITERS]


def fused_body(factors, heads, tails, values):
    shards = lax.axis_size(("ent", "blk"))
    z_count = lax.axis_size("rel")
    ent_dev, width = factors.shape
    triples = heads.shape[3]
    half = width // 2
    f32, bf16 = jnp.float32, jnp.bfloat16
    vmem = pl.BlockSpec(memory_space=pltpu.VMEM)
    out = pltpu.VMEM((1, width, width), f32)
    share = half // z_count
    return pl.pallas_call(
        functools.partial(
            fused_kernel, z_count, 1.0 / (ent_dev * shards), 1.0 / math.sqrt(shards * triples)
        ),
        out_shape=(out, out),
        in_specs=[pl.BlockSpec(memory_space=pl.ANY)] * 4,
        out_specs=(vmem, vmem),
        scratch_shapes=[
            pltpu.VMEM(factors.shape, bf16),
            pltpu.VMEM(heads.shape, jnp.int32),
            pltpu.VMEM(tails.shape, jnp.int32),
            pltpu.VMEM(values.shape, f32),
            pltpu.SMEM(heads.shape, jnp.int32),
            pltpu.SMEM(tails.shape, jnp.int32),
            pltpu.SemaphoreType.DMA((6,)),
            pltpu.SemaphoreType.REGULAR((max(z_count - 2, 1),)),
            pltpu.VMEM((ent_dev // tile_width, width, tile_width), bf16),
            pltpu.VMEM((width, triples), bf16),
            pltpu.VMEM((width, triples), bf16),
            pltpu.VMEM((width, width), f32),
            pltpu.VMEM((share, width), f32),
            pltpu.VMEM((2, share, width), f32),
            pltpu.VMEM((2, share, width), f32),
            pltpu.VMEM((z_count, share, width), f32),
            pltpu.VMEM((width, width), f32),
            pltpu.VMEM((2, half, width), f32),
            pltpu.VMEM((4, width, width), f32),
            pltpu.VMEM((4, width, width), f32),
            pltpu.VMEM((4, width, width), f32),
            pltpu.VMEM((2, half, width), f32),
            pltpu.VMEM((2, half, width), f32),
            pltpu.VMEM((2, half, width), f32),
            pltpu.VMEM((2, half, width), f32),
            pltpu.VMEM((ITERS + 1, width, width), f32),
            pltpu.VMEM((8, z_count, 1, 128), f32),
            pltpu.SemaphoreType.DMA((COPIES,)),
            pltpu.SemaphoreType.DMA((COPIES,)),
        ],
        compiler_params=pltpu.CompilerParams(collective_id=0, has_side_effects=True),
    )(factors, heads, tails, values)


def solution(mesh):
    placed = (
        P(("ent", "blk"), None),
        P(None, "rel", None, ("ent", "blk")),
        P(None, "rel", None, ("ent", "blk")),
        P(None, "rel", None, ("ent", "blk")),
    )
    sizes = dict(mesh.shape)
    fused = sizes["ent"] == 2 and sizes["blk"] == 4 and sizes["rel"] in (2, 4, 8)
    return jax.shard_map(
        fused_body if fused else body,
        mesh=mesh,
        in_specs=placed,
        out_specs=(P(("ent", "blk", "rel"), None, None), P(("ent", "blk", "rel"), None, None)),
        check_vma=False,
    )
```

profile of v0, /device:TPU:0, one launch (start us, length us, event | category | flops | bytes accessed | tf_op | source)
XLA Modules:
  0.0 37.1 jit_solution(11279253009447900689)
XLA Ops:
  0.6 35.1 %shard_map.59 = (f32[1,256,256]{2,1,0:T(8,128)S(1)}, f32[1,256,256]{2,1,0:T(8,128)S(1)}) custom-call(bf16[1024,256]{1,0:T(8,128)(2,1)} %factors_hbm.1, s32[8,1,1,1024]{3,2,1,0:T(1,128)} %heads_hbm.1, s32[8,1,1,1024]{3,2,1,0:T(1,128)} %tails_hbm.1, f32[8,1,1,1024]{3,2,1,0:T(1,128)} %values_hbm.1), custom_call_target="tpu_custom_call" | custom-call | tf_op jit(solution)/shard_map/pallas_call | solution.py:458
  35.7 0.7 %copy.8 = f32[1,256,256]{2,1,0:T(8,128)} copy(f32[1,256,256]{2,1,0:T(8,128)S(1)} %get-tuple-element.2) | data formatting | bytes 524288
  36.4 0.7 %copy.9 = f32[1,256,256]{2,1,0:T(8,128)} copy(f32[1,256,256]{2,1,0:T(8,128)S(1)} %get-tuple-element.3) | data formatting | bytes 524288
where the time goes:
time: 37.3 us; the launch traced here: 37.1 us
  Pallas kernels  35.1 us (94%)
  local copies, waits for them, and re-layouts  1.41 us (4%)
  between operations  0.64 us (2%)
    pallas_call x1, Pallas kernels, fused_body(): pl.pallas_call(functools.partial(fused_kernel, z_count, 1.0 / (ent_dev *...  35.1 us
    unnamed x2, local copies, waits for them, and re-layouts  1.41 us

commit v1 on v0

--- a/solution.py
+++ b/solution.py
@@ -115,18 +115,19 @@
 
 
 MESH = pl.DeviceIdType.MESH
-COPIES = 64
+COPIES = 24
 
 
 def fused_kernel(
     z_count, scale_gram, scale_target,
     factors_hbm, heads_hbm, tails_hbm, values_hbm,
     fit_ref, res_ref,
-    factors_ref, heads_ref, tails_ref, values_ref, head_ids, tail_ids, load_sem, ready,
+    factors_ref, heads_ref, tails_ref, values_ref, head_ids, tail_ids,
+    first_heads, first_tails, load_sem, ready,
     turned, left_rows, right_rows,
     gram_part, gram_in, gram_half, gram_xy, gram_line, gram_full, gram_pair,
     pair_out, pair_in, own_sum, first_a, first_b, second_a, second_b,
-    basis, table, send_sem, recv_sem,
+    basis, early, late, send_sem, recv_sem,
 ):
     f32, bf16 = jnp.float32, jnp.bfloat16
     width = factors_ref.shape[1]
@@ -170,15 +171,18 @@
     for peer in near:
         pl.semaphore_signal(barrier, inc=1, device_id=peer, device_id_type=MESH)
     tell(barrier)
+    first_q = (1 - e) * 4 + (1 - y) * 2 + 1 - c
     loads = []
     for slot, (source, dest) in enumerate(
         (
             (factors_hbm, factors_ref),
-            (heads_hbm, head_ids),
-            (tails_hbm, tail_ids),
+            (heads_hbm.at[pl.ds(first_q, 1)], first_heads),
+            (tails_hbm.at[pl.ds(first_q, 1)], first_tails),
             (heads_hbm, heads_ref),
             (values_hbm, values_ref),
             (tails_hbm, tails_ref),
+            (heads_hbm, head_ids),
+            (tails_hbm, tail_ids),
         )
     ):
         loads.append(pltpu.make_async_copy(source, dest, load_sem.at[slot]))
@@ -186,24 +190,39 @@
 
     counter = [0]
 
-    def send(source, dest, peer):
+    def spare():
         slot = counter[0]
         counter[0] += 1
-        copy = pltpu.make_async_remote_copy(
-            src_ref=source, dst_ref=dest,
-            send_sem=send_sem.at[slot], recv_sem=recv_sem.at[slot],
+        return send_sem.at[slot], recv_sem.at[slot]
+
+    def copy_to(source, dest, peer, pair):
+        return pltpu.make_async_remote_copy(
+            src_ref=source, dst_ref=dest, send_sem=pair[0], recv_sem=pair[1],
             device_id=peer, device_id_type=MESH,
         )
+
+    def send(source, dest, peer):
+        copy = copy_to(source, dest, peer, spare())
         copy.start()
         return copy
+
+    far_peers = [
+        (m, hop) for hop in range(z_count - 1, -1, -1) for m in (7, 6, 5, 3, 4, 2, 1, 0) if m or hop
+    ]
+
+    def spread(table):
+        pair = spare()
+        for m, hop in far_peers:
+            peer = group_peer(m)[:2] + (lax.rem(z + hop, z_count),)
+            place = m * z_count + (z_count - hop) % z_count
+            copy_to(table.at[0], table.at[place], peer, pair).start()
+        others = table.at[pl.ds(1, 8 * z_count - 1)]
+        return copy_to(others, others, pair_peer, pair)
 
     loads[0].wait()
     flipped = factors_ref[...].T
     for block in range(turned.shape[0]):
         turned[block] = flipped[:, block * tile_width : (block + 1) * tile_width]
-    gram_part[...] = lax.dot_general(
-        flipped, flipped, (((1,), (1,)), ((), ())), preferred_element_type=f32
-    )
     own_rows = pl.ds(pl.multiple_of(c * half, half), half)
     other_rows = pl.ds(pl.multiple_of((1 - c) * half, half), half)
     own_share = pl.ds(pl.multiple_of(c * half + z * share, share), share)
@@ -212,13 +231,13 @@
     row_number = lax.broadcasted_iota(jnp.int32, (tile_width, tile_width), 0)
     blank = jnp.zeros((tile_width, tile_width), bf16)
 
-    def gathered(ids_ref, scalar_ref, q, first):
+    def gathered(ids_ref, scalar_ref, q, place, first):
         picks, blocks = [], []
         for tile in (first, first + 1):
             start = tile * tile_width
             inside = lax.rem(ids_ref[q, 0, :, start : start + tile_width], tile_width)
             picks.append(jnp.where(row_number == inside, 1.0, 0.0).astype(bf16))
-            blocks.append(turned[lax.div(scalar_ref[q, 0, 0, start], tile_width)])
+            blocks.append(turned[lax.div(scalar_ref[place, 0, 0, start], tile_width)])
         mixed = jnp.concatenate(
             [
                 jnp.concatenate([picks[0], blank], axis=1),
@@ -228,13 +247,14 @@
         )
         return jnp.dot(jnp.concatenate(blocks, axis=1), mixed, preferred_element_type=f32)
 
-    def partial(pe, py, pc):
+    def partial(pe, py, pc, head_blocks=head_ids, tail_blocks=tail_ids, place=None):
         q = pe * 4 + py * 2 + pc
+        place = q if place is None else place
         for first in range(0, triples // tile_width, 2):
             cols = slice(first * tile_width, (first + 2) * tile_width)
-            rows = gathered(heads_ref, head_ids, q, first)
+            rows = gathered(heads_ref, head_blocks, q, place, first)
             left_rows[:, cols] = (values_ref[q, 0, :, cols] * rows).astype(bf16)
-            right_rows[:, cols] = gathered(tails_ref, tail_ids, q, first).astype(bf16)
+            right_rows[:, cols] = gathered(tails_ref, tail_blocks, q, place, first).astype(bf16)
         return lax.dot_general(
             left_rows[...], right_rows[...], (((1,), (1,)), ((), ())), preferred_element_type=f32
         )
@@ -250,37 +270,58 @@
     def keep(index):
         pe, py = targets[index]
         own_sum[index] = partial(pe, py, c)
+
+    def join(index):
         pair_copies[index].wait()
         own_sum[index] = own_sum[index] + pair_in[index]
 
     top, low = pl.ds(0, half), pl.ds(half, half)
-    for load in loads[1:]:
+    for load in loads[1:6]:
         load.wait()
-    pair_out[0] = partial(1 - e, 1 - y, 1 - c)
+    pair_out[0] = partial(1 - e, 1 - y, 1 - c, first_heads, first_tails, 0)
     pl.semaphore_wait(barrier, len(near) + line_count)
+    pair_copies.append(send(pair_out.at[0], pair_in.at[0], pair_peer))
+    if z_count > 2:
+        tell(ready.at[0])
+    gram_part[...] = lax.dot_general(
+        flipped, flipped, (((1,), (1,)), ((), ())), preferred_element_type=f32
+    )
     g_pair = send(gram_part.at[other_share], gram_in, pair_peer)
-    pair_copies.append(send(pair_out.at[0], pair_in.at[0], pair_peer))
-    for step in range(z_count - 2):
-        tell(ready.at[step])
-        if step + 1 < z_count - 2:
-            pl.semaphore_wait(ready.at[step], line_count)
+    for load in loads[6:]:
+        load.wait()
+    keep(0)
     g_pair.wait()
     gram_half[0] = gram_part[own_share, :] + gram_in[...]
     upper, lower = pl.ds(0, part), pl.ds(part, part)
     g_a1 = send(gram_half.at[0, upper], gram_xy.at[0, upper], x_peer)
     g_b1 = send(gram_half.at[0, lower], gram_xy.at[0, lower], y_peer)
-    keep(0)
+    join(0)
     a_diag = send(own_sum.at[0, top], first_a.at[0], x_peer)
     b_diag = send(own_sum.at[0, low], first_b.at[0], y_peer)
     give(1)
+    give(2)
+    for step in range(1, z_count - 2):
+        pl.semaphore_wait(ready.at[step - 1], line_count)
+        tell(ready.at[step])
+    keep(1)
     g_a1.wait()
     g_b1.wait()
     gram_half[1] = gram_half[0] + gram_xy[0]
     g_a2 = send(gram_half.at[1, upper], gram_xy.at[1, upper], y_peer)
     g_b2 = send(gram_half.at[1, lower], gram_xy.at[1, lower], x_peer)
-    keep(1)
+    join(1)
     a_side = send(own_sum.at[1, top], first_a.at[1], x_peer)
-    give(2)
+    keep(2)
+    join(2)
+    b_side = send(own_sum.at[2, low], first_b.at[1], y_peer)
+    give(3)
+    keep(3)
+    a_diag.wait()
+    second_a[0] = own_sum[2, :half, :] + first_a[0]
+    a_last = send(second_a.at[0], second_a.at[1], y_peer)
+    b_diag.wait()
+    second_b[0] = own_sum[1, half:, :] + first_b[0]
+    b_last = send(second_b.at[0], second_b.at[1], x_peer)
     g_a2.wait()
     g_b2.wait()
     gram_line[0] = gram_half[1] + gram_xy[1]
@@ -290,16 +331,7 @@
         send(gram_line.at[0], gram_line.at[z_count - hop], z_peer(hop))
         for hop in range(1, z_count)
     ]
-    keep(2)
-    b_side = send(own_sum.at[2, low], first_b.at[1], y_peer)
-    a_diag.wait()
-    second_a[0] = own_sum[2, :half, :] + first_a[0]
-    a_last = send(second_a.at[0], second_a.at[1], y_peer)
-    b_diag.wait()
-    second_b[0] = own_sum[1, half:, :] + first_b[0]
-    b_last = send(second_b.at[0], second_b.at[1], x_peer)
-    give(3)
-    keep(3)
+    join(3)
     for copy in line_copies:
         copy.wait()
     for hop in range(z_count):
@@ -309,10 +341,43 @@
     g_full.wait()
     gram_full[own_rows, :] = gram_pair[0] * scale_gram
     gram_full[other_rows, :] = gram_pair[1] * scale_gram
+
+    def split(value):
+        high = value.astype(bf16)
+        return high, (value - high.astype(f32)).astype(bf16)
+
+    def total(value):
+        return jnp.sum(jnp.sum(value, axis=0, keepdims=True), axis=1, keepdims=True)
+
+    def two_sided(matrix):
+        matrix_high, matrix_low = split(matrix)
+        matrix_both = jnp.concatenate([matrix_high, matrix_low], axis=0)
+
+        def apply(value):
+            high, low_part = split(value)
+            both = jnp.dot(matrix_both, high, preferred_element_type=f32)
+            inner = both[:width] + (
+                both[width:] + jnp.dot(matrix_high, low_part, preferred_element_type=f32)
+            )
+            high, low_part = split(inner)
+            both = jnp.dot(
+                jnp.concatenate([high, low_part], axis=0),
+                matrix_high,
+                preferred_element_type=f32,
+            )
+            return both[:width] + (
+                both[width:] + jnp.dot(high, matrix_low, preferred_element_type=f32)
+            )
+
+        return apply
+
     gram = gram_full[...]
-    gram_high = gram.astype(bf16)
-    gram_low = (gram - gram_high.astype(f32)).astype(bf16)
-    gram_both = jnp.concatenate([gram_high, gram_low], axis=0)
+    gram_high, gram_low = split(gram)
+    gram_twice = jnp.dot(gram_high, gram_high, preferred_element_type=f32) + (
+        jnp.dot(gram_high, gram_low, preferred_element_type=f32)
+        + jnp.dot(gram_low, gram_high, preferred_element_type=f32)
+    )
+    once, twice = two_sided(gram), two_sided(gram_twice)
     a_side.wait()
     b_side.wait()
     a_last.wait()
@@ -320,67 +385,59 @@
     basis[0, :half, :] = ((own_sum[3, :half, :] + first_a[1]) + second_a[1]) * scale_target
     basis[0, half:, :] = ((own_sum[3, half:, :] + first_b[1]) + second_b[1]) * scale_target
 
-    def split(value):
-        high = value.astype(bf16)
-        return high, (value - high.astype(f32)).astype(bf16)
-
-    def total(value):
-        return jnp.sum(jnp.sum(value, axis=0, keepdims=True), axis=1, keepdims=True)
-
-    def normal_map(value):
-        high, low_part = split(value)
-        both = jnp.dot(gram_both, high, preferred_element_type=f32)
-        inner = both[:width] + (
-            both[width:] + jnp.dot(gram_high, low_part, preferred_element_type=f32)
-        )
-        high, low_part = split(inner)
-        both = jnp.dot(
-            jnp.concatenate([high, low_part], axis=0), gram_high, preferred_element_type=f32
-        )
-        outer = both[:width] + (
-            both[width:] + jnp.dot(high, gram_low, preferred_element_type=f32)
-        )
-        return outer + ridge_weight * value
-
     lane = lax.broadcasted_iota(jnp.int32, (1, 128), 1)
     record = jnp.zeros((1, 128), f32)
+
+    def noted(record, place, value):
+        return jnp.where(lane == place, value, record)
+
+    def sized(vector):
+        square = total(vector * vector)
+        inverse = jnp.where(square > 0.0, lax.rsqrt(square), 0.0)
+        return inverse, square * inverse
+
     inverses = []
-    for index in range(ITERS):
+    for index in range(0, ITERS, 2):
         vector = basis[index]
-        image = normal_map(vector)
-        square = total(vector * vector)
-        cross = total(vector * image)
-        inverse = jnp.where(square > 0.0, lax.rsqrt(square), 0.0)
-        length = square * inverse
-        diagonal = (cross * inverse) * inverse
-        record = jnp.where(lane == index, diagonal, record)
-        record = jnp.where(lane == ITERS + index, length, record)
-        if index + 1 == ITERS:
-            table[0, 0] = record
-            far_copies = [
-                send(
-                    table.at[0, 0],
-                    table.at[m, (z_count - hop) % z_count],
-                    group_peer(m)[:2] + (lax.rem(z + hop, z_count),),
-                )
-                for hop in range(z_count)
-                for m in range(8)
-                if m or hop
-            ]
+        image = once(vector)
+        image_twice = twice(vector)
+        inverse, length = sized(vector)
+        record = noted(record, ITERS + index, length)
+        if index + 2 == ITERS:
+            early[0] = record
+            early_copy = spread(early)
+        diagonal = (total(vector * image) * inverse) * inverse
+        record = noted(record, index, diagonal + ridge_weight)
         following = (image - diagonal * vector) * inverse
+        beyond = (image_twice - diagonal * image) * inverse
         if index > 0:
-            following = following - (length * inverses[-1]) * basis[index - 1]
+            ratio = length * inverses[-1]
+            following = following - ratio * basis[index - 1]
+            beyond = beyond - ratio * mapped
+        mapped = beyond
         inverses.append(inverse)
         basis[index + 1] = following
-    for copy in far_copies:
-        copy.wait()
-
-    lines = table[...].reshape(8 * z_count, 128)
-    filled = jnp.concatenate([lines, jnp.zeros((128 - 8 * z_count, 128), f32)], axis=0).T
-    alpha = [filled[j : j + 1, :] for j in range(ITERS)]
-    beta = [filled[ITERS + j : ITERS + j + 1, :] for j in range(ITERS)] + [
-        jnp.ones((1, 128), f32)
-    ]
+        inverse, length = sized(following)
+        diagonal = (total(following * beyond) * inverse) * inverse
+        record = noted(record, index + 1, diagonal + ridge_weight)
+        record = noted(record, ITERS + index + 1, length)
+        if index + 2 == ITERS:
+            late[0] = record
+            late_copy = spread(late)
+        basis[index + 2] = (beyond - diagonal * following) * inverse - (
+            length * inverses[-1]
+        ) * vector
+        inverses.append(inverse)
+
+    def lanes_of(table):
+        lines = table[...].reshape(8 * z_count, 128)
+        blank_lines = jnp.zeros((128 - 8 * z_count, 128), f32)
+        return jnp.concatenate([lines, blank_lines], axis=0).T
+
+    early_copy.wait()
+    filled = lanes_of(early)
+    alpha = [filled[j : j + 1, :] for j in range(ITERS - 2)]
+    beta = [filled[ITERS + j : ITERS + j + 1, :] for j in range(ITERS - 1)]
 
     def reduced(rows):
         added = rows[0]
@@ -425,8 +482,13 @@
             for j, row in enumerate(along)
         ]
         if index + 1 < ITERS:
+            norm_next = reduced([row * row for row in residual])
+            if index + 3 == ITERS:
+                late_copy.wait()
+                filled = lanes_of(late)
+                alpha += [filled[j : j + 1, :] for j in range(ITERS - 2, ITERS)]
+                beta += [filled[2 * ITERS - 1 : 2 * ITERS, :], jnp.ones((1, 128), f32)]
             image = small_map(residual)
-            norm_next = reduced([row * row for row in residual])
             product = reduced([row * image[j] for j, row in enumerate(residual)])
             ratio = norm_next / norm_now
             step_size = norm_next / (product - ratio * norm_next / step_size)
@@ -469,7 +531,9 @@
             pltpu.VMEM(values.shape, f32),
             pltpu.SMEM(heads.shape, jnp.int32),
             pltpu.SMEM(tails.shape, jnp.int32),
-            pltpu.SemaphoreType.DMA((6,)),
+            pltpu.SMEM((1,) + heads.shape[1:], jnp.int32),
+            pltpu.SMEM((1,) + heads.shape[1:], jnp.int32),
+            pltpu.SemaphoreType.DMA((8,)),
             pltpu.SemaphoreType.REGULAR((max(z_count - 2, 1),)),
             pltpu.VMEM((ent_dev // tile_width, width, tile_width), bf16),
             pltpu.VMEM((width, triples), bf16),
@@ -489,7 +553,8 @@
             pltpu.VMEM((2, half, width), f32),
             pltpu.VMEM((2, half, width), f32),
             pltpu.VMEM((ITERS + 1, width, width), f32),
-            pltpu.VMEM((8, z_count, 1, 128), f32),
+            pltpu.VMEM((8 * z_count, 1, 128), f32),
+            pltpu.VMEM((8 * z_count, 1, 128), f32),
             pltpu.SemaphoreType.DMA((COPIES,)),
             pltpu.SemaphoreType.DMA((COPIES,)),
         ],

time: 37.3 us -> 30.9 us (0.83)
  Pallas kernels: 35.1 us -> 28.7 us
    pallas_call x1, Pallas kernels: 35.1 us -> 28.7 us  [fused_body(): pl.pallas_call(functools.partial(fused_kernel, z_count, 1.0 / (ent_dev *...]
where the time goes in v1:
time: 30.9 us; the launch traced here: 30.7 us
  Pallas kernels  28.7 us (93%)
  local copies, waits for them, and re-layouts  1.41 us (5%)
  between operations  0.64 us (2%)
    pallas_call x1, Pallas kernels, fused_body(): pl.pallas_call(functools.partial(fused_kernel, z_count, 1.0 / (ent_dev *...  28.7 us
    unnamed x2, local copies, waits for them, and re-layouts  1.41 us

profile of v1, /device:TPU:0, one launch (start us, length us, event | category | flops | bytes accessed | tf_op | source)
XLA Modules:
  0.0 30.7 jit_solution(1372381063418167574)
XLA Ops:
  0.6 28.7 %shard_map.59 = (f32[1,256,256]{2,1,0:T(8,128)S(1)}, f32[1,256,256]{2,1,0:T(8,128)S(1)}) custom-call(bf16[1024,256]{1,0:T(8,128)(2,1)} %factors_hbm.1, s32[8,1,1,1024]{3,2,1,0:T(1,128)} %heads_hbm.1, s32[8,1,1,1024]{3,2,1,0:T(1,128)} %tails_hbm.1, f32[8,1,1,1024]{3,2,1,0:T(1,128)} %values_hbm.1), custom_call_target="tpu_custom_call" | custom-call | tf_op jit(solution)/shard_map/pallas_call | solution.py:520
  29.3 0.7 %copy.8 = f32[1,256,256]{2,1,0:T(8,128)} copy(f32[1,256,256]{2,1,0:T(8,128)S(1)} %get-tuple-element.2) | data formatting | bytes 524288
  30.0 0.7 %copy.9 = f32[1,256,256]{2,1,0:T(8,128)} copy(f32[1,256,256]{2,1,0:T(8,128)S(1)} %get-tuple-element.3) | data formatting | bytes 524288

commit v2 on v1

--- a/solution.py
+++ b/solution.py
@@ -115,15 +115,17 @@
 
 
 MESH = pl.DeviceIdType.MESH
-COPIES = 24
+COPIES = 21
+CHUNKS = 4
+PIECES = 7
 
 
 def fused_kernel(
     z_count, scale_gram, scale_target,
     factors_hbm, heads_hbm, tails_hbm, values_hbm,
-    fit_ref, res_ref,
+    pieces, mix_ref,
     factors_ref, heads_ref, tails_ref, values_ref, head_ids, tail_ids,
-    first_heads, first_tails, load_sem, ready,
+    first_heads, first_tails, factor_sem, load_sem, ready,
     turned, left_rows, right_rows,
     gram_part, gram_in, gram_half, gram_xy, gram_line, gram_full, gram_pair,
     pair_out, pair_in, own_sum, first_a, first_b, second_a, second_b,
@@ -172,10 +174,19 @@
         pl.semaphore_signal(barrier, inc=1, device_id=peer, device_id_type=MESH)
     tell(barrier)
     first_q = (1 - e) * 4 + (1 - y) * 2 + 1 - c
+    chunk = factors_ref.shape[0] // CHUNKS
+    factor_loads = []
+    for slot in range(CHUNKS):
+        rows = pl.ds(slot * chunk, chunk)
+        factor_loads.append(
+            pltpu.make_async_copy(
+                factors_hbm.at[rows], factors_ref.at[rows], factor_sem.at[slot]
+            )
+        )
+        factor_loads[-1].start()
     loads = []
     for slot, (source, dest) in enumerate(
         (
-            (factors_hbm, factors_ref),
             (heads_hbm.at[pl.ds(first_q, 1)], first_heads),
             (tails_hbm.at[pl.ds(first_q, 1)], first_tails),
             (heads_hbm, heads_ref),
@@ -219,10 +230,14 @@
         others = table.at[pl.ds(1, 8 * z_count - 1)]
         return copy_to(others, others, pair_peer, pair)
 
-    loads[0].wait()
-    flipped = factors_ref[...].T
-    for block in range(turned.shape[0]):
-        turned[block] = flipped[:, block * tile_width : (block + 1) * tile_width]
+    flipped = []
+    for slot in range(CHUNKS):
+        factor_loads[slot].wait()
+        flipped.append(factors_ref[slot * chunk : (slot + 1) * chunk, :].T)
+        for step in range(chunk // tile_width):
+            turned[slot * (chunk // tile_width) + step] = flipped[-1][
+                :, step * tile_width : (step + 1) * tile_width
+            ]
     own_rows = pl.ds(pl.multiple_of(c * half, half), half)
     other_rows = pl.ds(pl.multiple_of((1 - c) * half, half), half)
     own_share = pl.ds(pl.multiple_of(c * half + z * share, share), share)
@@ -276,18 +291,18 @@
         own_sum[index] = own_sum[index] + pair_in[index]
 
     top, low = pl.ds(0, half), pl.ds(half, half)
-    for load in loads[1:6]:
+    for load in loads[:5]:
         load.wait()
     pair_out[0] = partial(1 - e, 1 - y, 1 - c, first_heads, first_tails, 0)
     pl.semaphore_wait(barrier, len(near) + line_count)
     pair_copies.append(send(pair_out.at[0], pair_in.at[0], pair_peer))
     if z_count > 2:
         tell(ready.at[0])
-    gram_part[...] = lax.dot_general(
-        flipped, flipped, (((1,), (1,)), ((), ())), preferred_element_type=f32
+    gram_part[...] = jnp.dot(
+        jnp.concatenate(flipped, axis=1), factors_ref[...], preferred_element_type=f32
     )
     g_pair = send(gram_part.at[other_share], gram_in, pair_peer)
-    for load in loads[6:]:
+    for load in loads[5:]:
         load.wait()
     keep(0)
     g_pair.wait()
@@ -396,18 +411,13 @@
         inverse = jnp.where(square > 0.0, lax.rsqrt(square), 0.0)
         return inverse, square * inverse
 
-    inverses = []
+    inverses, lengths, diagonals = [], [], []
     for index in range(0, ITERS, 2):
         vector = basis[index]
         image = once(vector)
         image_twice = twice(vector)
         inverse, length = sized(vector)
-        record = noted(record, ITERS + index, length)
-        if index + 2 == ITERS:
-            early[0] = record
-            early_copy = spread(early)
         diagonal = (total(vector * image) * inverse) * inverse
-        record = noted(record, index, diagonal + ridge_weight)
         following = (image - diagonal * vector) * inverse
         beyond = (image_twice - diagonal * image) * inverse
         if index > 0:
@@ -415,29 +425,30 @@
             following = following - ratio * basis[index - 1]
             beyond = beyond - ratio * mapped
         mapped = beyond
-        inverses.append(inverse)
         basis[index + 1] = following
-        inverse, length = sized(following)
-        diagonal = (total(following * beyond) * inverse) * inverse
-        record = noted(record, index + 1, diagonal + ridge_weight)
-        record = noted(record, ITERS + index + 1, length)
-        if index + 2 == ITERS:
-            late[0] = record
-            late_copy = spread(late)
-        basis[index + 2] = (beyond - diagonal * following) * inverse - (
-            length * inverses[-1]
+        next_inverse, next_length = sized(following)
+        next_diagonal = (total(following * beyond) * next_inverse) * next_inverse
+        basis[index + 2] = (beyond - next_diagonal * following) * next_inverse - (
+            next_length * inverse
         ) * vector
-        inverses.append(inverse)
+        inverses += [inverse, next_inverse]
+        lengths += [length, next_length]
+        diagonals += [diagonal + ridge_weight, next_diagonal + ridge_weight]
+        for place in (index, index + 1):
+            record = noted(record, place, diagonals[place])
+            record = noted(record, ITERS + place, lengths[place])
+        if index + 4 == ITERS:
+            early[0] = record
+            early_copy = spread(early)
+    late[0] = record
+    late_copy = spread(late)
+    inverses.append(jnp.ones((1, 1), f32))
+    lengths.append(jnp.ones((1, 1), f32))
 
     def lanes_of(table):
         lines = table[...].reshape(8 * z_count, 128)
         blank_lines = jnp.zeros((128 - 8 * z_count, 128), f32)
         return jnp.concatenate([lines, blank_lines], axis=0).T
-
-    early_copy.wait()
-    filled = lanes_of(early)
-    alpha = [filled[j : j + 1, :] for j in range(ITERS - 2)]
-    beta = [filled[ITERS + j : ITERS + j + 1, :] for j in range(ITERS - 1)]
 
     def reduced(rows):
         added = rows[0]
@@ -445,10 +456,10 @@
             added = added + row
         return jnp.sum(added, axis=1, keepdims=True)
 
-    def small_map(rows):
+    def small_map(rows, alpha, beta):
         count = len(rows)
         made = []
-        for j in range(count + 1):
+        for j in range(min(count + 1, len(beta))):
             entry = None
             if j < count:
                 entry = alpha[j] * rows[j]
@@ -465,46 +476,126 @@
             one + ratio * second[j] if j < len(second) else one for j, one in enumerate(first)
         ]
 
+    def products(residual, image):
+        return (
+            reduced([row * row for row in residual]),
+            reduced([row * image[j] for j, row in enumerate(residual)]),
+        )
+
+    early_copy.wait()
+    filled = lanes_of(early)
+    known = ITERS - 2
+    alpha = [filled[j : j + 1, :] for j in range(known)]
+    beta = [filled[ITERS + j : ITERS + j + 1, :] for j in range(known)]
     residual = [beta[0]]
-    image = small_map(residual)
-    norm_now = reduced([row * row for row in residual])
-    product = reduced([row * image[j] for j, row in enumerate(residual)])
+    image = small_map(residual, alpha, beta)
+    norm_now, product = products(residual, image)
     step_size = norm_now / product
     direction, along = residual, image
     fitted = []
-    for index in range(ITERS):
-        fitted = [
-            fitted[j] + step_size * row if j < len(fitted) else step_size * row
-            for j, row in enumerate(direction)
-        ]
+    for index in range(known):
+        if index == 0:
+            fitted = [step_size * row for row in direction]
+        else:
+            fitted = [
+                fitted[j] + step_size * row if j < len(fitted) else step_size * row
+                for j, row in enumerate(direction)
+            ]
         residual = [
             residual[j] - step_size * row if j < len(residual) else -(step_size * row)
             for j, row in enumerate(along)
         ]
-        if index + 1 < ITERS:
-            norm_next = reduced([row * row for row in residual])
-            if index + 3 == ITERS:
-                late_copy.wait()
-                filled = lanes_of(late)
-                alpha += [filled[j : j + 1, :] for j in range(ITERS - 2, ITERS)]
-                beta += [filled[2 * ITERS - 1 : 2 * ITERS, :], jnp.ones((1, 128), f32)]
-            image = small_map(residual)
-            product = reduced([row * image[j] for j, row in enumerate(residual)])
+        if index + 1 < known:
+            image = small_map(residual, alpha, beta)
+            norm_next, product = products(residual, image)
             ratio = norm_next / norm_now
             step_size = norm_next / (product - ratio * norm_next / step_size)
             direction = mixed_sum(residual, ratio, direction)
             along = mixed_sum(image, ratio, along)
             norm_now = norm_next
-    inverses.append(jnp.ones((1, 1), f32))
-    fit_weights = [row[:, 0:1] * inverses[j] for j, row in enumerate(fitted)]
-    res_weights = [row[:, 0:1] * inverses[j] for j, row in enumerate(residual)]
-    fit = fit_weights[0] * basis[0]
-    res = res_weights[0] * basis[0]
-    for j in range(1, ITERS):
-        fit = fit + fit_weights[j] * basis[j]
-        res = res + res_weights[j] * basis[j]
-    fit_ref[0] = fit
-    res_ref[0] = res + res_weights[ITERS] * basis[ITERS]
+
+    def own(rows):
+        return [row[:, 0:1] for row in rows]
+
+    own_step = step_size[:, 0:1]
+    own_direction = own(direction)
+    own_along = own(along) + [lengths[known] * own_direction[-1]]
+    own_residual = own(residual) + [-(own_step * own_along[-1])]
+    own_image = small_map(own_residual, diagonals, lengths)
+    weight_sets = (
+        own(fitted),
+        own_direction,
+        own_residual,
+        own_along,
+        own_image,
+        small_map(own_along, diagonals, lengths),
+        small_map(own_image, diagonals, lengths),
+    )
+    for place, weights in enumerate(weight_sets):
+        added = (weights[0] * inverses[0]) * basis[0]
+        for j in range(1, len(weights)):
+            added = added + (weights[j] * inverses[j]) * basis[j]
+        pieces[place] = added
+
+    late_copy.wait()
+    filled = lanes_of(late)
+    alpha += [filled[j : j + 1, :] for j in range(known, ITERS)]
+    beta += [filled[ITERS + j : ITERS + j + 1, :] for j in range(known, ITERS)]
+    beta.append(jnp.ones((1, 128), f32))
+    along = along + [beta[known] * direction[-1]]
+    residual = residual + [-(step_size * along[-1])]
+    image = small_map(residual, alpha, beta)
+    norm_next, product = products(residual, image)
+    ratio = norm_next / norm_now
+    step_next = norm_next / (product - ratio * norm_next / step_size)
+    residual = [
+        residual[j] - step_next * row if j < len(residual) else -(step_next * row)
+        for j, row in enumerate(mixed_sum(image, ratio, along))
+    ]
+    norm_last, product = products(residual, small_map(residual, alpha, beta))
+    ratio_last = norm_last / norm_next
+    step_last = norm_last / (product - ratio_last * norm_last / step_next)
+    longer = step_next + step_last * ratio_last
+    both_steps = step_last * step_next
+    for place, value in enumerate(
+        (longer + step_last, longer * ratio, both_steps, both_steps * ratio)
+    ):
+        mix_ref[place : place + 1, :] = jnp.broadcast_to(value, (1, 128))
+
+
+def finish_kernel(pieces, mix_ref, fit_hbm, res_hbm, fit_rows, res_rows, fit_sem, res_sem):
+    mixes = [mix_ref[place : place + 1, 0:1] for place in range(4)]
+    height = fit_rows.shape[0] // CHUNKS
+    copies = []
+    for slot in range(CHUNKS):
+        rows = pl.ds(slot * height, height)
+        fitted, direction, residual, along, image, second_along, second_image = [
+            pieces[place, slot * height : (slot + 1) * height, :] for place in range(PIECES)
+        ]
+        fit_rows[rows, :] = (
+            fitted
+            + mixes[0] * residual
+            + mixes[1] * direction
+            - mixes[2] * image
+            - mixes[3] * along
+        )
+        copies.append(
+            pltpu.make_async_copy(fit_rows.at[rows], fit_hbm.at[0, rows], fit_sem.at[slot])
+        )
+        copies[-1].start()
+        res_rows[rows, :] = (
+            residual
+            - mixes[0] * image
+            - mixes[1] * along
+            + mixes[2] * second_image
+            + mixes[3] * second_along
+        )
+        copies.append(
+            pltpu.make_async_copy(res_rows.at[rows], res_hbm.at[0, rows], res_sem.at[slot])
+        )
+        copies[-1].start()
+    for copy in copies:
+        copy.wait()
 
 
 def fused_body(factors, heads, tails, values):
@@ -515,13 +606,12 @@
     half = width // 2
     f32, bf16 = jnp.float32, jnp.bfloat16
     vmem = pl.BlockSpec(memory_space=pltpu.VMEM)
-    out = pltpu.VMEM((1, width, width), f32)
     share = half // z_count
-    return pl.pallas_call(
+    pieces, mix = pl.pallas_call(
         functools.partial(
             fused_kernel, z_count, 1.0 / (ent_dev * shards), 1.0 / math.sqrt(shards * triples)
         ),
-        out_shape=(out, out),
+        out_shape=(pltpu.VMEM((PIECES, width, width), f32), pltpu.VMEM((8, 128), f32)),
         in_specs=[pl.BlockSpec(memory_space=pl.ANY)] * 4,
         out_specs=(vmem, vmem),
         scratch_shapes=[
@@ -533,7 +623,8 @@
             pltpu.SMEM(tails.shape, jnp.int32),
             pltpu.SMEM((1,) + heads.shape[1:], jnp.int32),
             pltpu.SMEM((1,) + heads.shape[1:], jnp.int32),
-            pltpu.SemaphoreType.DMA((8,)),
+            pltpu.SemaphoreType.DMA((CHUNKS,)),
+            pltpu.SemaphoreType.DMA((7,)),
             pltpu.SemaphoreType.REGULAR((max(z_count - 2, 1),)),
             pltpu.VMEM((ent_dev // tile_width, width, tile_width), bf16),
             pltpu.VMEM((width, triples), bf16),
@@ -560,6 +651,21 @@
         ],
         compiler_params=pltpu.CompilerParams(collective_id=0, has_side_effects=True),
     )(factors, heads, tails, values)
+    out = jax.ShapeDtypeStruct((1, width, width), f32)
+    anywhere = pl.BlockSpec(memory_space=pl.ANY)
+    return pl.pallas_call(
+        finish_kernel,
+        out_shape=(out, out),
+        in_specs=[vmem, vmem],
+        out_specs=(anywhere, anywhere),
+        scratch_shapes=[
+            pltpu.VMEM((width, width), f32),
+            pltpu.VMEM((width, width), f32),
+            pltpu.SemaphoreType.DMA((CHUNKS,)),
+            pltpu.SemaphoreType.DMA((CHUNKS,)),
+        ],
+        compiler_params=pltpu.CompilerParams(vmem_limit_bytes=16 * width * width * 4),
+    )(pieces, mix)
 
 
 def solution(mesh):

time: 30.9 us -> 31.3 us (1.013)
  Pallas kernels: 28.7 us -> 30.5 us
  local copies, waits for them, and re-layouts: 1.41 us -> 0 us
    unnamed x2 -> x0, local copies, waits for them, and re-layouts: 1.41 us -> none
    pallas_call x1, Pallas kernels: 28.7 us -> 29.6 us  [fused_body(): pl.pallas_call(functools.partial(fused_kernel, z_count, 1.0 / (ent_dev *...]
    pallas_call x0 -> x1, Pallas kernels: none -> 0.91 us  [fused_body(): pl.pallas_call(finish_kernel, out_shape=(out, out), in_specs=[vmem, vmem]...]
where the time goes in v2:
time: 31.3 us; the launch traced here: 31.2 us
  Pallas kernels  30.5 us (97%)
  between operations  0.64 us (2%)
    pallas_call x1, Pallas kernels, fused_body(): pl.pallas_call(functools.partial(fused_kernel, z_count, 1.0 / (ent_dev *...  29.6 us
    pallas_call x1, Pallas kernels, fused_body(): pl.pallas_call(finish_kernel, out_shape=(out, out), in_specs=[vmem, vmem]...  0.91 us

profile of v2, /device:TPU:0, one launch (start us, length us, event | category | flops | bytes accessed | tf_op | source)
XLA Modules:
  0.0 31.2 jit_solution(9155721789323035576)
XLA Ops:
  0.6 29.6 %shard_map.59 = (f32[7,256,256]{2,1,0:T(8,128)S(1)}, f32[8,128]{1,0:T(8,128)S(1)}) custom-call(bf16[1024,256]{1,0:T(8,128)(2,1)} %factors_hbm.1, s32[8,1,1,1024]{3,2,1,0:T(1,128)} %heads_hbm.1, s32[8,1,1,1024]{3,2,1,0:T(1,128)} %tails_hbm.1, f32[8,1,1,1024]{3,2,1,0:T(1,128)} %values_hbm.1), custom_call_target="tpu_custom_call" | custom-call | tf_op jit(solution)/shard_map/pallas_call | solution.py:610
  30.3 0.9 %shard_map.60 = (f32[1,256,256]{2,1,0:T(8,128)}, f32[1,256,256]{2,1,0:T(8,128)}) custom-call(f32[7,256,256]{2,1,0:T(8,128)S(1)} %get-tuple-element.4.pieces, f32[8,128]{1,0:T(8,128)S(1)} %get-tuple-element.5.mix_ref), custom_call_target="tpu_custom_call" | custom-call | tf_op jit(solution)/shard_map/pallas_call | solution.py:656

commit v3 on v2

--- a/solution.py
+++ b/solution.py
@@ -117,19 +117,19 @@
 MESH = pl.DeviceIdType.MESH
 COPIES = 21
 CHUNKS = 4
-PIECES = 7
+STRIP = 32
 
 
 def fused_kernel(
     z_count, scale_gram, scale_target,
     factors_hbm, heads_hbm, tails_hbm, values_hbm,
-    pieces, mix_ref,
+    basis, mix_ref,
     factors_ref, heads_ref, tails_ref, values_ref, head_ids, tail_ids,
     first_heads, first_tails, factor_sem, load_sem, ready,
     turned, left_rows, right_rows,
     gram_part, gram_in, gram_half, gram_xy, gram_line, gram_full, gram_pair,
     pair_out, pair_in, own_sum, first_a, first_b, second_a, second_b,
-    basis, early, late, send_sem, recv_sem,
+    early, late, send_sem, recv_sem,
 ):
     f32, bf16 = jnp.float32, jnp.bfloat16
     width = factors_ref.shape[1]
@@ -218,7 +218,7 @@
         return copy
 
     far_peers = [
-        (m, hop) for hop in range(z_count - 1, -1, -1) for m in (7, 6, 5, 3, 4, 2, 1, 0) if m or hop
+        (m, hop) for hop in (*range(1, z_count), 0) for m in (7, 6, 5, 3, 4, 2, 1, 0) if m or hop
     ]
 
     def spread(table):
@@ -368,13 +368,15 @@
         matrix_high, matrix_low = split(matrix)
         matrix_both = jnp.concatenate([matrix_high, matrix_low], axis=0)
 
-        def apply(value):
+        def left(value):
             high, low_part = split(value)
             both = jnp.dot(matrix_both, high, preferred_element_type=f32)
-            inner = both[:width] + (
+            return both[:width] + (
                 both[width:] + jnp.dot(matrix_high, low_part, preferred_element_type=f32)
             )
-            high, low_part = split(inner)
+
+        def right(value):
+            high, low_part = split(value)
             both = jnp.dot(
                 jnp.concatenate([high, low_part], axis=0),
                 matrix_high,
@@ -384,7 +386,7 @@
                 both[width:] + jnp.dot(high, matrix_low, preferred_element_type=f32)
             )
 
-        return apply
+        return left, right
 
     gram = gram_full[...]
     gram_high, gram_low = split(gram)
@@ -396,7 +398,7 @@
     a_side.wait()
     b_side.wait()
     a_last.wait()
-    b_last.wait()
+    b_last.wait_recv()
     basis[0, :half, :] = ((own_sum[3, :half, :] + first_a[1]) + second_a[1]) * scale_target
     basis[0, half:, :] = ((own_sum[3, half:, :] + first_b[1]) + second_b[1]) * scale_target
 
@@ -414,8 +416,10 @@
     inverses, lengths, diagonals = [], [], []
     for index in range(0, ITERS, 2):
         vector = basis[index]
-        image = once(vector)
-        image_twice = twice(vector)
+        inner, inner_twice = once[0](vector), twice[0](vector)
+        if index + 2 == ITERS:
+            b_last.wait_send()
+        image, image_twice = once[1](inner), twice[1](inner_twice)
         inverse, length = sized(vector)
         diagonal = (total(vector * image) * inverse) * inverse
         following = (image - diagonal * vector) * inverse
@@ -514,29 +518,6 @@
             along = mixed_sum(image, ratio, along)
             norm_now = norm_next
 
-    def own(rows):
-        return [row[:, 0:1] for row in rows]
-
-    own_step = step_size[:, 0:1]
-    own_direction = own(direction)
-    own_along = own(along) + [lengths[known] * own_direction[-1]]
-    own_residual = own(residual) + [-(own_step * own_along[-1])]
-    own_image = small_map(own_residual, diagonals, lengths)
-    weight_sets = (
-        own(fitted),
-        own_direction,
-        own_residual,
-        own_along,
-        own_image,
-        small_map(own_along, diagonals, lengths),
-        small_map(own_image, diagonals, lengths),
-    )
-    for place, weights in enumerate(weight_sets):
-        added = (weights[0] * inverses[0]) * basis[0]
-        for j in range(1, len(weights)):
-            added = added + (weights[j] * inverses[j]) * basis[j]
-        pieces[place] = added
-
     late_copy.wait()
     filled = lanes_of(late)
     alpha += [filled[j : j + 1, :] for j in range(known, ITERS)]
@@ -548,52 +529,57 @@
     norm_next, product = products(residual, image)
     ratio = norm_next / norm_now
     step_next = norm_next / (product - ratio * norm_next / step_size)
+    residual_before, image_before = residual, image
     residual = [
         residual[j] - step_next * row if j < len(residual) else -(step_next * row)
         for j, row in enumerate(mixed_sum(image, ratio, along))
     ]
-    norm_last, product = products(residual, small_map(residual, alpha, beta))
+    fitted = [
+        fitted[j] + step_next * row if j < len(fitted) else step_next * row
+        for j, row in enumerate(mixed_sum(residual_before, ratio, direction))
+    ]
+    image = small_map(residual, alpha, beta)
+    norm_last, product = products(residual, image)
     ratio_last = norm_last / norm_next
     step_last = norm_last / (product - ratio_last * norm_last / step_next)
-    longer = step_next + step_last * ratio_last
-    both_steps = step_last * step_next
-    for place, value in enumerate(
-        (longer + step_last, longer * ratio, both_steps, both_steps * ratio)
-    ):
-        mix_ref[place : place + 1, :] = jnp.broadcast_to(value, (1, 128))
-
-
-def finish_kernel(pieces, mix_ref, fit_hbm, res_hbm, fit_rows, res_rows, fit_sem, res_sem):
-    mixes = [mix_ref[place : place + 1, 0:1] for place in range(4)]
+    direction = mixed_sum(residual, ratio_last, mixed_sum(residual_before, ratio, direction))
+    along = mixed_sum(image, ratio_last, mixed_sum(image_before, ratio, along))
+    fitted = [
+        fitted[j] + step_last * row if j < len(fitted) else step_last * row
+        for j, row in enumerate(direction)
+    ]
+    residual = [
+        residual[j] - step_last * row if j < len(residual) else -(step_last * row)
+        for j, row in enumerate(along)
+    ]
+    for place, row in enumerate(fitted + residual):
+        weight = row[:, 0:1] * inverses[place if place < ITERS else place - ITERS]
+        mix_ref[place : place + 1, :] = jnp.broadcast_to(weight, (1, width))
+
+
+def finish_kernel(basis, mix_ref, fit_hbm, res_hbm, fit_rows, res_rows, fit_sem, res_sem):
+    count = basis.shape[0] - 1
+    weights = [mix_ref[place : place + 1, :] for place in range(2 * count + 1)]
     height = fit_rows.shape[0] // CHUNKS
     copies = []
     for slot in range(CHUNKS):
+        for first in range(slot * height, (slot + 1) * height, STRIP):
+            strip = slice(first, first + STRIP)
+            vector = basis[0, strip, :]
+            fit, res = weights[0] * vector, weights[count] * vector
+            for j in range(1, count + 1):
+                vector = basis[j, strip, :]
+                res = res + weights[count + j] * vector
+                if j < count:
+                    fit = fit + weights[j] * vector
+            fit_rows[strip, :] = fit
+            res_rows[strip, :] = res
         rows = pl.ds(slot * height, height)
-        fitted, direction, residual, along, image, second_along, second_image = [
-            pieces[place, slot * height : (slot + 1) * height, :] for place in range(PIECES)
-        ]
-        fit_rows[rows, :] = (
-            fitted
-            + mixes[0] * residual
-            + mixes[1] * direction
-            - mixes[2] * image
-            - mixes[3] * along
-        )
-        copies.append(
-            pltpu.make_async_copy(fit_rows.at[rows], fit_hbm.at[0, rows], fit_sem.at[slot])
-        )
-        copies[-1].start()
-        res_rows[rows, :] = (
-            residual
-            - mixes[0] * image
-            - mixes[1] * along
-            + mixes[2] * second_image
-            + mixes[3] * second_along
-        )
-        copies.append(
-            pltpu.make_async_copy(res_rows.at[rows], res_hbm.at[0, rows], res_sem.at[slot])
-        )
-        copies[-1].start()
+        for source, dest, sem in ((fit_rows, fit_hbm, fit_sem), (res_rows, res_hbm, res_sem)):
+            copies.append(
+                pltpu.make_async_copy(source.at[rows], dest.at[0, rows], sem.at[slot])
+            )
+            copies[-1].start()
     for copy in copies:
         copy.wait()
 
@@ -607,11 +593,14 @@
     f32, bf16 = jnp.float32, jnp.bfloat16
     vmem = pl.BlockSpec(memory_space=pltpu.VMEM)
     share = half // z_count
-    pieces, mix = pl.pallas_call(
+    basis, mix = pl.pallas_call(
         functools.partial(
             fused_kernel, z_count, 1.0 / (ent_dev * shards), 1.0 / math.sqrt(shards * triples)
         ),
-        out_shape=(pltpu.VMEM((PIECES, width, width), f32), pltpu.VMEM((8, 128), f32)),
+        out_shape=(
+            pltpu.VMEM((ITERS + 1, width, width), f32),
+            pltpu.VMEM((3 * ITERS, width), f32),
+        ),
         in_specs=[pl.BlockSpec(memory_space=pl.ANY)] * 4,
         out_specs=(vmem, vmem),
         scratch_shapes=[
@@ -643,7 +632,6 @@
             pltpu.VMEM((2, half, width), f32),
             pltpu.VMEM((2, half, width), f32),
             pltpu.VMEM((2, half, width), f32),
-            pltpu.VMEM((ITERS + 1, width, width), f32),
             pltpu.VMEM((8 * z_count, 1, 128), f32),
             pltpu.VMEM((8 * z_count, 1, 128), f32),
             pltpu.SemaphoreType.DMA((COPIES,)),
@@ -665,7 +653,7 @@
             pltpu.SemaphoreType.DMA((CHUNKS,)),
         ],
         compiler_params=pltpu.CompilerParams(vmem_limit_bytes=16 * width * width * 4),
-    )(pieces, mix)
+    )(basis, mix)
 
 
 def solution(mesh):

time: 31.3 us -> 30.1 us (0.962)
  Pallas kernels: 30.5 us -> 29.3 us
    pallas_call x1, Pallas kernels: 29.6 us -> 28.3 us  [fused_body(): pl.pallas_call(functools.partial(fused_kernel, z_count, 1.0 / (ent_dev *...]
where the time goes in v3:
time: 30.1 us; the launch traced here: 29.9 us
  Pallas kernels  29.3 us (97%)
  between operations  0.64 us (2%)
    pallas_call x1, Pallas kernels, fused_body(): pl.pallas_call(functools.partial(fused_kernel, z_count, 1.0 / (ent_dev *...  28.3 us
    pallas_call x1, Pallas kernels, fused_body(): pl.pallas_call(finish_kernel, out_shape=(out, out), in_specs=[vmem, vmem]...  1 us

profile of v3, /device:TPU:0, one launch (start us, length us, event | category | flops | bytes accessed | tf_op | source)
XLA Modules:
  0.0 29.9 jit_solution(13827430827391168917)
XLA Ops:
  0.6 28.3 %shard_map.59 = (f32[9,256,256]{2,1,0:T(8,128)S(1)}, f32[24,256]{1,0:T(8,128)S(1)}) custom-call(bf16[1024,256]{1,0:T(8,128)(2,1)} %factors_hbm.1, s32[8,1,1,1024]{3,2,1,0:T(1,128)} %heads_hbm.1, s32[8,1,1,1024]{3,2,1,0:T(1,128)} %tails_hbm.1, f32[8,1,1,1024]{3,2,1,0:T(1,128)} %values_hbm.1), custom_call_target="tpu_custom_call" | custom-call | tf_op jit(solution)/shard_map/pallas_call | solution.py:596
  28.9 1.0 %shard_map.60 = (f32[1,256,256]{2,1,0:T(8,128)}, f32[1,256,256]{2,1,0:T(8,128)}) custom-call(f32[9,256,256]{2,1,0:T(8,128)S(1)} %get-tuple-element.4.basis, f32[24,256]{1,0:T(8,128)S(1)} %get-tuple-element.5.mix_ref), custom_call_target="tpu_custom_call" | custom-call | tf_op jit(solution)/shard_map/pallas_call | solution.py:644

commit v4 on v3

--- a/solution.py
+++ b/solution.py
@@ -118,6 +118,7 @@
 COPIES = 21
 CHUNKS = 4
 STRIP = 32
+PANEL = 128
 
 
 def fused_kernel(
@@ -129,6 +130,7 @@
     turned, left_rows, right_rows,
     gram_part, gram_in, gram_half, gram_xy, gram_line, gram_full, gram_pair,
     pair_out, pair_in, own_sum, first_a, first_b, second_a, second_b,
+    factor_left, factor_right, vector_parts, inner_parts, image, image_twice, mapped,
     early, late, send_sem, recv_sem,
 ):
     f32, bf16 = jnp.float32, jnp.bfloat16
@@ -361,46 +363,49 @@
         high = value.astype(bf16)
         return high, (value - high.astype(f32)).astype(bf16)
 
-    def total(value):
-        return jnp.sum(jnp.sum(value, axis=0, keepdims=True), axis=1, keepdims=True)
-
-    def two_sided(matrix):
-        matrix_high, matrix_low = split(matrix)
-        matrix_both = jnp.concatenate([matrix_high, matrix_low], axis=0)
-
-        def left(value):
-            high, low_part = split(value)
-            both = jnp.dot(matrix_both, high, preferred_element_type=f32)
-            return both[:width] + (
-                both[width:] + jnp.dot(matrix_high, low_part, preferred_element_type=f32)
-            )
-
-        def right(value):
-            high, low_part = split(value)
-            both = jnp.dot(
-                jnp.concatenate([high, low_part], axis=0),
-                matrix_high,
-                preferred_element_type=f32,
-            )
-            return both[:width] + (
-                both[width:] + jnp.dot(high, matrix_low, preferred_element_type=f32)
-            )
-
-        return left, right
-
+    def fold(value):
+        return jnp.sum(value.reshape(-1, 8, value.shape[1]), axis=0)
+
+    def total(parts):
+        added = parts[0]
+        for piece in parts[1:]:
+            added = added + piece
+        return jnp.sum(jnp.sum(added, axis=0, keepdims=True), axis=1, keepdims=True)
+
+    strips = [slice(first, first + STRIP) for first in range(0, width, STRIP)]
+    panels = range(0, width, PANEL)
     gram = gram_full[...]
     gram_high, gram_low = split(gram)
     gram_twice = jnp.dot(gram_high, gram_high, preferred_element_type=f32) + (
         jnp.dot(gram_high, gram_low, preferred_element_type=f32)
         + jnp.dot(gram_low, gram_high, preferred_element_type=f32)
     )
-    once, twice = two_sided(gram), two_sided(gram_twice)
+    for power, (high, low_part) in enumerate(((gram_high, gram_low), split(gram_twice))):
+        for third, piece in enumerate((high, low_part, high)):
+            span = slice(third * width, (third + 1) * width)
+            factor_left[power, :, span] = piece
+            factor_right[power, span, :] = piece
+
+    def spread_out(strip, value):
+        high, low_part = split(value)
+        for third, piece in enumerate((high, high, low_part)):
+            vector_parts[
+                slice(third * width + strip.start, third * width + strip.stop), :
+            ] = piece
+        return fold(value * value)
+
     a_side.wait()
     b_side.wait()
-    a_last.wait()
+    a_last.wait_recv()
     b_last.wait_recv()
-    basis[0, :half, :] = ((own_sum[3, :half, :] + first_a[1]) + second_a[1]) * scale_target
-    basis[0, half:, :] = ((own_sum[3, half:, :] + first_b[1]) + second_b[1]) * scale_target
+    squares = []
+    for strip in strips:
+        later = strip.start >= half
+        inside = slice(strip.start - half, strip.stop - half) if later else strip
+        side, last = (first_b, second_b) if later else (first_a, second_a)
+        value = ((own_sum[3, strip, :] + side[1, inside, :]) + last[1, inside, :]) * scale_target
+        basis[0, strip, :] = value
+        squares.append(spread_out(strip, value))
 
     lane = lax.broadcasted_iota(jnp.int32, (1, 128), 1)
     record = jnp.zeros((1, 128), f32)
@@ -408,33 +413,55 @@
     def noted(record, place, value):
         return jnp.where(lane == place, value, record)
 
-    def sized(vector):
-        square = total(vector * vector)
+    def sized(square):
         inverse = jnp.where(square > 0.0, lax.rsqrt(square), 0.0)
         return inverse, square * inverse
 
     inverses, lengths, diagonals = [], [], []
     for index in range(0, ITERS, 2):
-        vector = basis[index]
-        inner, inner_twice = once[0](vector), twice[0](vector)
+        for power in (0, 1):
+            for first in panels:
+                inner = jnp.dot(
+                    factor_left[power, first : first + PANEL, :],
+                    vector_parts[...],
+                    preferred_element_type=f32,
+                )
+                for step in range(0, PANEL, STRIP):
+                    high, low_part = split(inner[step : step + STRIP])
+                    rows = slice(first + step, first + step + STRIP)
+                    for third, piece in enumerate((high, high, low_part)):
+                        inner_parts[power, rows, third * width : (third + 1) * width] = piece
         if index + 2 == ITERS:
             b_last.wait_send()
-        image, image_twice = once[1](inner), twice[1](inner_twice)
-        inverse, length = sized(vector)
-        diagonal = (total(vector * image) * inverse) * inverse
-        following = (image - diagonal * vector) * inverse
-        beyond = (image_twice - diagonal * image) * inverse
-        if index > 0:
-            ratio = length * inverses[-1]
-            following = following - ratio * basis[index - 1]
-            beyond = beyond - ratio * mapped
-        mapped = beyond
-        basis[index + 1] = following
-        next_inverse, next_length = sized(following)
-        next_diagonal = (total(following * beyond) * next_inverse) * next_inverse
-        basis[index + 2] = (beyond - next_diagonal * following) * next_inverse - (
-            next_length * inverse
-        ) * vector
+        crosses = []
+        for power, dest in ((0, image), (1, image_twice)):
+            for first in panels:
+                outer = jnp.dot(
+                    inner_parts[power, first : first + PANEL, :],
+                    factor_right[power],
+                    preferred_element_type=f32,
+                )
+                dest[first : first + PANEL, :] = outer
+                for step in range(0, PANEL, STRIP):
+                    if power == 0:
+                        rows = slice(first + step, first + step + STRIP)
+                        crosses.append(fold(outer[step : step + STRIP] * basis[index, rows, :]))
+        inverse, length = sized(total(squares))
+        diagonal = (total(crosses) * inverse) * inverse
+        scaled = diagonal * inverse
+        ratio = length * inverses[-1] if index > 0 else None
+        squares, crosses = [], []
+        for strip in strips:
+            value = image[strip, :] * inverse - scaled * basis[index, strip, :]
+            if index > 0:
+                value = value - ratio * basis[index - 1, strip, :]
+            basis[index + 1, strip, :] = value
+            squares.append(fold(value * value))
+            crosses.append(fold(value * image_twice[strip, :]))
+        next_inverse, next_length = sized(total(squares))
+        next_diagonal = (
+            ((total(crosses) * inverse) * next_inverse) * next_inverse - diagonal
+        )
         inverses += [inverse, next_inverse]
         lengths += [length, next_length]
         diagonals += [diagonal + ridge_weight, next_diagonal + ridge_weight]
@@ -444,10 +471,26 @@
         if index + 4 == ITERS:
             early[0] = record
             early_copy = spread(early)
-    late[0] = record
-    late_copy = spread(late)
+        if index + 2 == ITERS:
+            late[0] = record
+            late_copy = spread(late)
+            a_last.wait_send()
+        now, before = (index // 2) % 2, (index // 2 + 1) % 2
+        for strip in strips:
+            value = image_twice[strip, :] * inverse - scaled * image[strip, :]
+            if index > 0:
+                value = value - ratio * mapped[before, strip, :]
+            mapped[now, strip, :] = value
+        next_scaled, next_ratio = next_diagonal * next_inverse, next_length * inverse
+        squares = []
+        for strip in strips:
+            value = (
+                mapped[now, strip, :] * next_inverse - next_ratio * basis[index, strip, :]
+            ) - next_scaled * basis[index + 1, strip, :]
+            basis[index + 2, strip, :] = value
+            if index + 2 < ITERS:
+                squares.append(spread_out(strip, value))
     inverses.append(jnp.ones((1, 1), f32))
-    lengths.append(jnp.ones((1, 1), f32))
 
     def lanes_of(table):
         lines = table[...].reshape(8 * z_count, 128)
@@ -632,6 +675,13 @@
             pltpu.VMEM((2, half, width), f32),
             pltpu.VMEM((2, half, width), f32),
             pltpu.VMEM((2, half, width), f32),
+            pltpu.VMEM((2, width, 3 * width), bf16),
+            pltpu.VMEM((2, 3 * width, width), bf16),
+            pltpu.VMEM((3 * width, width), bf16),
+            pltpu.VMEM((2, width, 3 * width), bf16),
+            pltpu.VMEM((width, width), f32),
+            pltpu.VMEM((width, width), f32),
+            pltpu.VMEM((2, width, width), f32),
             pltpu.VMEM((8 * z_count, 1, 128), f32),
             pltpu.VMEM((8 * z_count, 1, 128), f32),
             pltpu.SemaphoreType.DMA((COPIES,)),

time: 30.1 us -> 29.3 us (0.973)
  Pallas kernels: 29.3 us -> 28.5 us
    pallas_call x1, Pallas kernels: 28.3 us -> 27.5 us  [fused_body(): pl.pallas_call(functools.partial(fused_kernel, z_count, 1.0 / (ent_dev *...]
where the time goes in v4:
time: 29.3 us; the launch traced here: 29.1 us
  Pallas kernels  28.5 us (97%)
  between operations  0.64 us (2%)
    pallas_call x1, Pallas kernels, fused_body(): pl.pallas_call(functools.partial(fused_kernel, z_count, 1.0 / (ent_dev *...  27.5 us
    pallas_call x1, Pallas kernels, fused_body(): pl.pallas_call(finish_kernel, out_shape=(out, out), in_specs=[vmem, vmem]...  1 us

profile of v4, /device:TPU:0, one launch (start us, length us, event | category | flops | bytes accessed | tf_op | source)
XLA Modules:
  0.0 29.1 jit_solution(6139715232612124499)
XLA Ops:
  0.6 27.5 %shard_map.59 = (f32[9,256,256]{2,1,0:T(8,128)S(1)}, f32[24,256]{1,0:T(8,128)S(1)}) custom-call(bf16[1024,256]{1,0:T(8,128)(2,1)} %factors_hbm.1, s32[8,1,1,1024]{3,2,1,0:T(1,128)} %heads_hbm.1, s32[8,1,1,1024]{3,2,1,0:T(1,128)} %tails_hbm.1, f32[8,1,1,1024]{3,2,1,0:T(1,128)} %values_hbm.1), custom_call_target="tpu_custom_call" | custom-call | tf_op jit(solution)/shard_map/pallas_call | solution.py:639
  28.1 1.0 %shard_map.60 = (f32[1,256,256]{2,1,0:T(8,128)}, f32[1,256,256]{2,1,0:T(8,128)}) custom-call(f32[9,256,256]{2,1,0:T(8,128)S(1)} %get-tuple-element.4.basis, f32[24,256]{1,0:T(8,128)S(1)} %get-tuple-element.5.mix_ref), custom_call_target="tpu_custom_call" | custom-call | tf_op jit(solution)/shard_map/pallas_call | solution.py:694

commit v5 on v4

--- a/solution.py
+++ b/solution.py
@@ -451,17 +451,20 @@
         scaled = diagonal * inverse
         ratio = length * inverses[-1] if index > 0 else None
         squares, crosses = [], []
+        now, before = (index // 2) % 2, (index // 2 + 1) % 2
         for strip in strips:
             value = image[strip, :] * inverse - scaled * basis[index, strip, :]
             if index > 0:
                 value = value - ratio * basis[index - 1, strip, :]
             basis[index + 1, strip, :] = value
             squares.append(fold(value * value))
-            crosses.append(fold(value * image_twice[strip, :]))
+            beyond = image_twice[strip, :] * inverse - scaled * image[strip, :]
+            if index > 0:
+                beyond = beyond - ratio * mapped[before, strip, :]
+            mapped[now, strip, :] = beyond
+            crosses.append(fold(value * beyond))
         next_inverse, next_length = sized(total(squares))
-        next_diagonal = (
-            ((total(crosses) * inverse) * next_inverse) * next_inverse - diagonal
-        )
+        next_diagonal = (total(crosses) * next_inverse) * next_inverse
         inverses += [inverse, next_inverse]
         lengths += [length, next_length]
         diagonals += [diagonal + ridge_weight, next_diagonal + ridge_weight]
@@ -475,12 +478,6 @@
             late[0] = record
             late_copy = spread(late)
             a_last.wait_send()
-        now, before = (index // 2) % 2, (index // 2 + 1) % 2
-        for strip in strips:
-            value = image_twice[strip, :] * inverse - scaled * image[strip, :]
-            if index > 0:
-                value = value - ratio * mapped[before, strip, :]
-            mapped[now, strip, :] = value
         next_scaled, next_ratio = next_diagonal * next_inverse, next_length * inverse
         squares = []
         for strip in strips:
@@ -642,7 +639,7 @@
         ),
         out_shape=(
             pltpu.VMEM((ITERS + 1, width, width), f32),
-            pltpu.VMEM((3 * ITERS, width), f32),
+            pltpu.VMEM((4 * ITERS, width), f32),
         ),
         in_specs=[pl.BlockSpec(memory_space=pl.ANY)] * 4,
         out_specs=(vmem, vmem),

time: 29.3 us -> 29.3 us (level)
  no operation moved by 1% of the time
where the time goes in v5:
time: 29.3 us; the launch traced here: 29.1 us
  Pallas kernels  28.5 us (97%)
  between operations  0.64 us (2%)
    pallas_call x1, Pallas kernels, fused_body(): pl.pallas_call(functools.partial(fused_kernel, z_count, 1.0 / (ent_dev *...  27.5 us
    pallas_call x1, Pallas kernels, fused_body(): pl.pallas_call(finish_kernel, out_shape=(out, out), in_specs=[vmem, vmem]...  1 us

profile of v5, /device:TPU:0, one launch (start us, length us, event | category | flops | bytes accessed | tf_op | source)
XLA Modules:
  0.0 29.1 jit_solution(2368090382113209355)
XLA Ops:
  0.6 27.5 %shard_map.59 = (f32[9,256,256]{2,1,0:T(8,128)S(1)}, f32[32,256]{1,0:T(8,128)S(1)}) custom-call(bf16[1024,256]{1,0:T(8,128)(2,1)} %factors_hbm.1, s32[8,1,1,1024]{3,2,1,0:T(1,128)} %heads_hbm.1, s32[8,1,1,1024]{3,2,1,0:T(1,128)} %tails_hbm.1, f32[8,1,1,1024]{3,2,1,0:T(1,128)} %values_hbm.1), custom_call_target="tpu_custom_call" | custom-call | tf_op jit(solution)/shard_map/pallas_call | solution.py:636
  28.1 1.0 %shard_map.60 = (f32[1,256,256]{2,1,0:T(8,128)}, f32[1,256,256]{2,1,0:T(8,128)}) custom-call(f32[9,256,256]{2,1,0:T(8,128)S(1)} %get-tuple-element.4.basis, f32[32,256]{1,0:T(8,128)S(1)} %get-tuple-element.5.mix_ref), custom_call_target="tpu_custom_call" | custom-call | tf_op jit(solution)/shard_map/pallas_call | solution.py:691

commit v6 on v5

--- a/solution.py
+++ b/solution.py
@@ -115,7 +115,7 @@
 
 
 MESH = pl.DeviceIdType.MESH
-COPIES = 21
+COPIES = 24
 CHUNKS = 4
 STRIP = 32
 PANEL = 128
@@ -124,7 +124,7 @@
 def fused_kernel(
     z_count, scale_gram, scale_target,
     factors_hbm, heads_hbm, tails_hbm, values_hbm,
-    basis, mix_ref,
+    basis, mix_ref, scale_ref,
     factors_ref, heads_ref, tails_ref, values_ref, head_ids, tail_ids,
     first_heads, first_tails, factor_sem, load_sem, ready,
     turned, left_rows, right_rows,
@@ -134,7 +134,7 @@
     early, late, send_sem, recv_sem,
 ):
     f32, bf16 = jnp.float32, jnp.bfloat16
-    width = factors_ref.shape[1]
+    width = factors_ref.shape[2]
     half = width // 2
     share = half // z_count
     part = share // 2
@@ -176,13 +176,13 @@
         pl.semaphore_signal(barrier, inc=1, device_id=peer, device_id_type=MESH)
     tell(barrier)
     first_q = (1 - e) * 4 + (1 - y) * 2 + 1 - c
-    chunk = factors_ref.shape[0] // CHUNKS
+    block_count = factors_ref.shape[0]
     factor_loads = []
-    for slot in range(CHUNKS):
-        rows = pl.ds(slot * chunk, chunk)
+    for block in range(block_count):
+        rows = pl.ds(block * tile_width, tile_width)
         factor_loads.append(
             pltpu.make_async_copy(
-                factors_hbm.at[rows], factors_ref.at[rows], factor_sem.at[slot]
+                factors_hbm.at[rows], factors_ref.at[block], factor_sem.at[block]
             )
         )
         factor_loads[-1].start()
@@ -202,6 +202,7 @@
         loads[-1].start()
 
     counter = [0]
+    sent = []
 
     def spare():
         slot = counter[0]
@@ -217,6 +218,7 @@
     def send(source, dest, peer):
         copy = copy_to(source, dest, peer, spare())
         copy.start()
+        sent.append(copy)
         return copy
 
     far_peers = [
@@ -233,13 +235,10 @@
         return copy_to(others, others, pair_peer, pair)
 
     flipped = []
-    for slot in range(CHUNKS):
-        factor_loads[slot].wait()
-        flipped.append(factors_ref[slot * chunk : (slot + 1) * chunk, :].T)
-        for step in range(chunk // tile_width):
-            turned[slot * (chunk // tile_width) + step] = flipped[-1][
-                :, step * tile_width : (step + 1) * tile_width
-            ]
+    for block in range(block_count):
+        factor_loads[block].wait()
+        flipped.append(factors_ref[block].T)
+        turned[block] = flipped[-1]
     own_rows = pl.ds(pl.multiple_of(c * half, half), half)
     other_rows = pl.ds(pl.multiple_of((1 - c) * half, half), half)
     own_share = pl.ds(pl.multiple_of(c * half + z * share, share), share)
@@ -248,99 +247,139 @@
     row_number = lax.broadcasted_iota(jnp.int32, (tile_width, tile_width), 0)
     blank = jnp.zeros((tile_width, tile_width), bf16)
 
-    def gathered(ids_ref, scalar_ref, q, place, first):
-        picks, blocks = [], []
+    top, low = slice(0, half), slice(half, width)
+
+    def by_halves(left, right):
+        return jnp.concatenate(
+            [
+                jnp.dot(left[rows], right, preferred_element_type=f32)
+                for rows in (slice(0, half), slice(half, width))
+            ],
+            axis=0,
+        )
+
+    def picked(ids_ref, q, first):
+        picks = []
         for tile in (first, first + 1):
             start = tile * tile_width
             inside = lax.rem(ids_ref[q, 0, :, start : start + tile_width], tile_width)
             picks.append(jnp.where(row_number == inside, 1.0, 0.0).astype(bf16))
-            blocks.append(turned[lax.div(scalar_ref[place, 0, 0, start], tile_width)])
-        mixed = jnp.concatenate(
+        return picks
+
+    def paired(picks):
+        return jnp.concatenate(
             [
                 jnp.concatenate([picks[0], blank], axis=1),
                 jnp.concatenate([blank, picks[1]], axis=1),
             ],
             axis=0,
         )
-        return jnp.dot(jnp.concatenate(blocks, axis=1), mixed, preferred_element_type=f32)
+
+    def block_of(scalar_ref, place, tile):
+        return lax.div(scalar_ref[place, 0, 0, tile * tile_width], tile_width)
 
     def partial(pe, py, pc, head_blocks=head_ids, tail_blocks=tail_ids, place=None):
         q = pe * 4 + py * 2 + pc
         place = q if place is None else place
         for first in range(0, triples // tile_width, 2):
             cols = slice(first * tile_width, (first + 2) * tile_width)
-            rows = gathered(heads_ref, head_blocks, q, place, first)
+            picks = picked(heads_ref, q, first)
+            blocks = [turned[block_of(head_blocks, place, tile)] for tile in (first, first + 1)]
+            rows = jnp.dot(
+                jnp.concatenate(blocks, axis=1), paired(picks), preferred_element_type=f32
+            )
             left_rows[:, cols] = (values_ref[q, 0, :, cols] * rows).astype(bf16)
-            right_rows[:, cols] = gathered(tails_ref, tail_blocks, q, place, first).astype(bf16)
-        return lax.dot_general(
-            left_rows[...], right_rows[...], (((1,), (1,)), ((), ())), preferred_element_type=f32
-        )
+            picks = [pick.T for pick in picked(tails_ref, q, first)]
+            blocks = [
+                factors_ref[block_of(tail_blocks, place, tile)] for tile in (first, first + 1)
+            ]
+            right_rows[cols, :] = jnp.dot(
+                paired(picks), jnp.concatenate(blocks, axis=0), preferred_element_type=f32
+            ).astype(bf16)
+        return [
+            jnp.dot(left_rows[rows, :], right_rows[...], preferred_element_type=f32)
+            for rows in (top, low)
+        ]
 
     targets = ((1 - e, 1 - y), (1 - e, y), (e, 1 - y), (e, y))
     pair_copies = []
 
     def give(index):
         pe, py = targets[index]
-        pair_out[index] = partial(pe, py, 1 - c)
+        pair_out[index, top], pair_out[index, low] = partial(pe, py, 1 - c)
         pair_copies.append(send(pair_out.at[index], pair_in.at[index], pair_peer))
 
     def keep(index):
         pe, py = targets[index]
-        own_sum[index] = partial(pe, py, c)
+        own_sum[index, top], own_sum[index, low] = partial(pe, py, c)
 
     def join(index):
-        pair_copies[index].wait()
+        pair_copies[index].wait_recv()
         own_sum[index] = own_sum[index] + pair_in[index]
 
-    top, low = pl.ds(0, half), pl.ds(half, half)
     for load in loads[:5]:
         load.wait()
-    pair_out[0] = partial(1 - e, 1 - y, 1 - c, first_heads, first_tails, 0)
+    pair_out[0, top], pair_out[0, low] = partial(
+        1 - e, 1 - y, 1 - c, first_heads, first_tails, 0
+    )
     pl.semaphore_wait(barrier, len(near) + line_count)
-    pair_copies.append(send(pair_out.at[0], pair_in.at[0], pair_peer))
+    pair_top = send(pair_out.at[0, pl.ds(0, half)], pair_in.at[0, pl.ds(0, half)], pair_peer)
+    pair_low = send(pair_out.at[0, pl.ds(half, half)], pair_in.at[0, pl.ds(half, half)], pair_peer)
+    pair_copies.append(None)
     if z_count > 2:
         tell(ready.at[0])
-    gram_part[...] = jnp.dot(
-        jnp.concatenate(flipped, axis=1), factors_ref[...], preferred_element_type=f32
+    gram_part[...] = by_halves(
+        jnp.concatenate(flipped, axis=1),
+        jnp.concatenate([factors_ref[block] for block in range(block_count)], axis=0),
     )
     g_pair = send(gram_part.at[other_share], gram_in, pair_peer)
     for load in loads[5:]:
         load.wait()
     keep(0)
-    g_pair.wait()
+    lead, rest = pl.ds(0, half // 2), pl.ds(half // 2, half // 2)
+    pair_top.wait_recv()
+    own_sum[0, top] = own_sum[0, top] + pair_in[0, top]
+    diag_copies = [send(own_sum.at[0, lead], first_a.at[0, lead], x_peer)]
+    pair_low.wait_recv()
+    own_sum[0, low] = own_sum[0, low] + pair_in[0, low]
+    diag_copies.append(
+        send(own_sum.at[0, pl.ds(half, half // 2)], first_b.at[0, lead], y_peer)
+    )
+    g_pair.wait_recv()
     gram_half[0] = gram_part[own_share, :] + gram_in[...]
     upper, lower = pl.ds(0, part), pl.ds(part, part)
     g_a1 = send(gram_half.at[0, upper], gram_xy.at[0, upper], x_peer)
     g_b1 = send(gram_half.at[0, lower], gram_xy.at[0, lower], y_peer)
-    join(0)
-    a_diag = send(own_sum.at[0, top], first_a.at[0], x_peer)
-    b_diag = send(own_sum.at[0, low], first_b.at[0], y_peer)
+    a_diag = send(own_sum.at[0, rest], first_a.at[0, rest], x_peer)
+    b_diag = send(own_sum.at[0, pl.ds(half + half // 2, half // 2)], first_b.at[0, rest], y_peer)
     give(1)
     give(2)
     for step in range(1, z_count - 2):
         pl.semaphore_wait(ready.at[step - 1], line_count)
         tell(ready.at[step])
     keep(1)
-    g_a1.wait()
-    g_b1.wait()
+    g_a1.wait_recv()
+    g_b1.wait_recv()
     gram_half[1] = gram_half[0] + gram_xy[0]
     g_a2 = send(gram_half.at[1, upper], gram_xy.at[1, upper], y_peer)
     g_b2 = send(gram_half.at[1, lower], gram_xy.at[1, lower], x_peer)
     join(1)
-    a_side = send(own_sum.at[1, top], first_a.at[1], x_peer)
+    a_side = send(own_sum.at[1, pl.ds(0, half)], first_a.at[1], x_peer)
     keep(2)
     join(2)
-    b_side = send(own_sum.at[2, low], first_b.at[1], y_peer)
+    b_side = send(own_sum.at[2, pl.ds(half, half)], first_b.at[1], y_peer)
     give(3)
     keep(3)
-    a_diag.wait()
+    diag_copies[0].wait_recv()
+    a_diag.wait_recv()
     second_a[0] = own_sum[2, :half, :] + first_a[0]
     a_last = send(second_a.at[0], second_a.at[1], y_peer)
-    b_diag.wait()
+    diag_copies[1].wait_recv()
+    b_diag.wait_recv()
     second_b[0] = own_sum[1, half:, :] + first_b[0]
     b_last = send(second_b.at[0], second_b.at[1], x_peer)
-    g_a2.wait()
-    g_b2.wait()
+    g_a2.wait_recv()
+    g_b2.wait_recv()
     gram_line[0] = gram_half[1] + gram_xy[1]
     if z_count > 2:
         pl.semaphore_wait(ready.at[z_count - 3], line_count)
@@ -350,12 +389,12 @@
     ]
     join(3)
     for copy in line_copies:
-        copy.wait()
+        copy.wait_recv()
     for hop in range(z_count):
         place = lax.rem(z + hop, z_count)
         gram_pair[0, pl.ds(pl.multiple_of(place * share, share), share), :] = gram_line[hop]
     g_full = send(gram_pair.at[0], gram_pair.at[1], pair_peer)
-    g_full.wait()
+    g_full.wait_recv()
     gram_full[own_rows, :] = gram_pair[0] * scale_gram
     gram_full[other_rows, :] = gram_pair[1] * scale_gram
 
@@ -394,8 +433,8 @@
             ] = piece
         return fold(value * value)
 
-    a_side.wait()
-    b_side.wait()
+    a_side.wait_recv()
+    b_side.wait_recv()
     a_last.wait_recv()
     b_last.wait_recv()
     squares = []
@@ -448,17 +487,19 @@
                         crosses.append(fold(outer[step : step + STRIP] * basis[index, rows, :]))
         inverse, length = sized(total(squares))
         diagonal = (total(crosses) * inverse) * inverse
+        ready_now = diagonal == diagonal
+        step_inverse = inverse
         scaled = diagonal * inverse
         ratio = length * inverses[-1] if index > 0 else None
         squares, crosses = [], []
         now, before = (index // 2) % 2, (index // 2 + 1) % 2
         for strip in strips:
-            value = image[strip, :] * inverse - scaled * basis[index, strip, :]
+            value = image[strip, :] * step_inverse - scaled * basis[index, strip, :]
             if index > 0:
                 value = value - ratio * basis[index - 1, strip, :]
             basis[index + 1, strip, :] = value
             squares.append(fold(value * value))
-            beyond = image_twice[strip, :] * inverse - scaled * image[strip, :]
+            beyond = image_twice[strip, :] * step_inverse - scaled * image[strip, :]
             if index > 0:
                 beyond = beyond - ratio * mapped[before, strip, :]
             mapped[now, strip, :] = beyond
@@ -488,6 +529,9 @@
             if index + 2 < ITERS:
                 squares.append(spread_out(strip, value))
     inverses.append(jnp.ones((1, 1), f32))
+    for copy in sent:
+        if copy is not a_last and copy is not b_last:
+            copy.wait_send()
 
     def lanes_of(table):
         lines = table[...].reshape(8 * z_count, 128)
@@ -526,6 +570,9 @@
             reduced([row * image[j] for j, row in enumerate(residual)]),
         )
 
+    for place in range(2 * ITERS + 1):
+        inverse = inverses[place if place < ITERS else place - ITERS]
+        scale_ref[place : place + 1, :] = jnp.broadcast_to(inverse, (1, 128))
     early_copy.wait()
     filled = lanes_of(early)
     known = ITERS - 2
@@ -593,13 +640,17 @@
         for j, row in enumerate(along)
     ]
     for place, row in enumerate(fitted + residual):
-        weight = row[:, 0:1] * inverses[place if place < ITERS else place - ITERS]
-        mix_ref[place : place + 1, :] = jnp.broadcast_to(weight, (1, width))
-
-
-def finish_kernel(basis, mix_ref, fit_hbm, res_hbm, fit_rows, res_rows, fit_sem, res_sem):
+        mix_ref[place : place + 1, :] = row
+
+
+def finish_kernel(
+    basis, mix_ref, scale_ref, fit_hbm, res_hbm, fit_rows, res_rows, fit_sem, res_sem
+):
     count = basis.shape[0] - 1
-    weights = [mix_ref[place : place + 1, :] for place in range(2 * count + 1)]
+    width = basis.shape[2]
+    own_weights = mix_ref[0 : 2 * count + 1, 0:1] * scale_ref[0 : 2 * count + 1, 0:1]
+    spread_weights = jnp.broadcast_to(own_weights, (2 * count + 1, width))
+    weights = [spread_weights[place : place + 1, :] for place in range(2 * count + 1)]
     height = fit_rows.shape[0] // CHUNKS
     copies = []
     for slot in range(CHUNKS):
@@ -633,18 +684,19 @@
     f32, bf16 = jnp.float32, jnp.bfloat16
     vmem = pl.BlockSpec(memory_space=pltpu.VMEM)
     share = half // z_count
-    basis, mix = pl.pallas_call(
+    basis, mix, scale = pl.pallas_call(
         functools.partial(
             fused_kernel, z_count, 1.0 / (ent_dev * shards), 1.0 / math.sqrt(shards * triples)
         ),
         out_shape=(
             pltpu.VMEM((ITERS + 1, width, width), f32),
-            pltpu.VMEM((4 * ITERS, width), f32),
+            pltpu.VMEM((4 * ITERS, 128), f32),
+            pltpu.VMEM((4 * ITERS, 128), f32),
         ),
         in_specs=[pl.BlockSpec(memory_space=pl.ANY)] * 4,
-        out_specs=(vmem, vmem),
+        out_specs=(vmem, vmem, vmem),
         scratch_shapes=[
-            pltpu.VMEM(factors.shape, bf16),
+            pltpu.VMEM((ent_dev // tile_width, tile_width, width), bf16),
             pltpu.VMEM(heads.shape, jnp.int32),
             pltpu.VMEM(tails.shape, jnp.int32),
             pltpu.VMEM(values.shape, f32),
@@ -652,12 +704,12 @@
             pltpu.SMEM(tails.shape, jnp.int32),
             pltpu.SMEM((1,) + heads.shape[1:], jnp.int32),
             pltpu.SMEM((1,) + heads.shape[1:], jnp.int32),
-            pltpu.SemaphoreType.DMA((CHUNKS,)),
+            pltpu.SemaphoreType.DMA((ent_dev // tile_width,)),
             pltpu.SemaphoreType.DMA((7,)),
             pltpu.SemaphoreType.REGULAR((max(z_count - 2, 1),)),
             pltpu.VMEM((ent_dev // tile_width, width, tile_width), bf16),
             pltpu.VMEM((width, triples), bf16),
-            pltpu.VMEM((width, triples), bf16),
+            pltpu.VMEM((triples, width), bf16),
             pltpu.VMEM((width, width), f32),
             pltpu.VMEM((share, width), f32),
             pltpu.VMEM((2, share, width), f32),
@@ -691,7 +743,7 @@
     return pl.pallas_call(
         finish_kernel,
         out_shape=(out, out),
-        in_specs=[vmem, vmem],
+        in_specs=[vmem, vmem, vmem],
         out_specs=(anywhere, anywhere),
         scratch_shapes=[
             pltpu.VMEM((width, width), f32),
@@ -700,7 +752,7 @@
             pltpu.SemaphoreType.DMA((CHUNKS,)),
         ],
         compiler_params=pltpu.CompilerParams(vmem_limit_bytes=16 * width * width * 4),
-    )(basis, mix)
+    )(basis, mix, scale)
 
 
 def solution(mesh):

time: 29.3 us -> 30.7 us (1.048)
  Pallas kernels: 28.5 us -> 29.9 us
    pallas_call x1, Pallas kernels: 27.5 us -> 28.8 us  [fused_body(): pl.pallas_call(functools.partial(fused_kernel, z_count, 1.0 / (ent_dev *...]
where the time goes in v6:
time: 30.7 us; the launch traced here: 30.5 us
  Pallas kernels  29.9 us (97%)
  between operations  0.64 us (2%)
    pallas_call x1, Pallas kernels, fused_body(): pl.pallas_call(functools.partial(fused_kernel, z_count, 1.0 / (ent_dev *...  28.8 us
    pallas_call x1, Pallas kernels, fused_body(): pl.pallas_call(finish_kernel, out_shape=(out, out), in_specs=[vmem, vmem,...  1.04 us

profile of v6, /device:TPU:0, one launch (start us, length us, event | category | flops | bytes accessed | tf_op | source)
XLA Modules:
  0.0 30.5 jit_solution(13145549343193105547)
XLA Ops:
  0.6 28.8 %shard_map.59 = (f32[9,256,256]{2,1,0:T(8,128)S(1)}, f32[32,128]{1,0:T(8,128)S(1)}, f32[32,128]{1,0:T(8,128)S(1)}) custom-call(bf16[1024,256]{1,0:T(8,128)(2,1)} %factors_hbm.1, s32[8,1,1,1024]{3,2,1,0:T(1,128)} %heads_hbm.1, s32[8,1,1,1024]{3,2,1,0:T(1,128)} %tails_hbm.1, f32[8,1,1,1024]{3,2,1,0:T(1,128)} %values_hbm.1), custom_call_target="tpu_custom_call" | custom-call | tf_op jit(solution)/shard_map/pallas_call | solution.py:687
  29.5 1.0 %shard_map.60 = (f32[1,256,256]{2,1,0:T(8,128)}, f32[1,256,256]{2,1,0:T(8,128)}) custom-call(f32[9,256,256]{2,1,0:T(8,128)S(1)} %get-tuple-element.5.basis, f32[32,128]{1,0:T(8,128)S(1)} %get-tuple-element.6.mix_ref, f32[32,128]{1,0:T(8,128)S(1)} %get-tuple-element.7.scale_ref), custom_call_target="tpu_custom_call" | custom-call | tf_op jit(solution)/shard_map/pallas_call | solution.py:743

commit v7 on v6

--- a/solution.py
+++ b/solution.py
@@ -115,7 +115,7 @@
 
 
 MESH = pl.DeviceIdType.MESH
-COPIES = 24
+COPIES = 22
 CHUNKS = 4
 STRIP = 32
 PANEL = 128
@@ -336,22 +336,17 @@
     for load in loads[5:]:
         load.wait()
     keep(0)
-    lead, rest = pl.ds(0, half // 2), pl.ds(half // 2, half // 2)
-    pair_top.wait_recv()
-    own_sum[0, top] = own_sum[0, top] + pair_in[0, top]
-    diag_copies = [send(own_sum.at[0, lead], first_a.at[0, lead], x_peer)]
-    pair_low.wait_recv()
-    own_sum[0, low] = own_sum[0, low] + pair_in[0, low]
-    diag_copies.append(
-        send(own_sum.at[0, pl.ds(half, half // 2)], first_b.at[0, lead], y_peer)
-    )
     g_pair.wait_recv()
     gram_half[0] = gram_part[own_share, :] + gram_in[...]
     upper, lower = pl.ds(0, part), pl.ds(part, part)
     g_a1 = send(gram_half.at[0, upper], gram_xy.at[0, upper], x_peer)
     g_b1 = send(gram_half.at[0, lower], gram_xy.at[0, lower], y_peer)
-    a_diag = send(own_sum.at[0, rest], first_a.at[0, rest], x_peer)
-    b_diag = send(own_sum.at[0, pl.ds(half + half // 2, half // 2)], first_b.at[0, rest], y_peer)
+    pair_top.wait_recv()
+    own_sum[0, top] = own_sum[0, top] + pair_in[0, top]
+    a_diag = send(own_sum.at[0, pl.ds(0, half)], first_a.at[0], x_peer)
+    pair_low.wait_recv()
+    own_sum[0, low] = own_sum[0, low] + pair_in[0, low]
+    b_diag = send(own_sum.at[0, pl.ds(half, half)], first_b.at[0], y_peer)
     give(1)
     give(2)
     for step in range(1, z_count - 2):
@@ -370,11 +365,9 @@
     b_side = send(own_sum.at[2, pl.ds(half, half)], first_b.at[1], y_peer)
     give(3)
     keep(3)
-    diag_copies[0].wait_recv()
     a_diag.wait_recv()
     second_a[0] = own_sum[2, :half, :] + first_a[0]
     a_last = send(second_a.at[0], second_a.at[1], y_peer)
-    diag_copies[1].wait_recv()
     b_diag.wait_recv()
     second_b[0] = own_sum[1, half:, :] + first_b[0]
     b_last = send(second_b.at[0], second_b.at[1], x_peer)

time: 30.7 us -> 29.3 us (0.954)
  Pallas kernels: 29.9 us -> 28.5 us
    pallas_call x1, Pallas kernels: 28.8 us -> 27.5 us  [fused_body(): pl.pallas_call(functools.partial(fused_kernel, z_count, 1.0 / (ent_dev *...]
where the time goes in v7:
time: 29.3 us; the launch traced here: 29.2 us
  Pallas kernels  28.5 us (97%)
  between operations  0.64 us (2%)
    pallas_call x1, Pallas kernels, fused_body(): pl.pallas_call(functools.partial(fused_kernel, z_count, 1.0 / (ent_dev *...  27.5 us
    pallas_call x1, Pallas kernels, fused_body(): pl.pallas_call(finish_kernel, out_shape=(out, out), in_specs=[vmem, vmem,...  1.04 us

profile of v7, /device:TPU:0, one launch (start us, length us, event | category | flops | bytes accessed | tf_op | source)
XLA Modules:
  0.0 29.2 jit_solution(10346008506997489605)
XLA Ops:
  0.6 27.5 %shard_map.59 = (f32[9,256,256]{2,1,0:T(8,128)S(1)}, f32[32,128]{1,0:T(8,128)S(1)}, f32[32,128]{1,0:T(8,128)S(1)}) custom-call(bf16[1024,256]{1,0:T(8,128)(2,1)} %factors_hbm.1, s32[8,1,1,1024]{3,2,1,0:T(1,128)} %heads_hbm.1, s32[8,1,1,1024]{3,2,1,0:T(1,128)} %tails_hbm.1, f32[8,1,1,1024]{3,2,1,0:T(1,128)} %values_hbm.1), custom_call_target="tpu_custom_call" | custom-call | tf_op jit(solution)/shard_map/pallas_call | solution.py:680
  28.1 1.0 %shard_map.60 = (f32[1,256,256]{2,1,0:T(8,128)}, f32[1,256,256]{2,1,0:T(8,128)}) custom-call(f32[9,256,256]{2,1,0:T(8,128)S(1)} %get-tuple-element.5.basis, f32[32,128]{1,0:T(8,128)S(1)} %get-tuple-element.6.mix_ref, f32[32,128]{1,0:T(8,128)S(1)} %get-tuple-element.7.scale_ref), custom_call_target="tpu_custom_call" | custom-call | tf_op jit(solution)/shard_map/pallas_call | solution.py:736

commit v8 on v7

--- a/solution.py
+++ b/solution.py
@@ -130,7 +130,7 @@
     turned, left_rows, right_rows,
     gram_part, gram_in, gram_half, gram_xy, gram_line, gram_full, gram_pair,
     pair_out, pair_in, own_sum, first_a, first_b, second_a, second_b,
-    factor_left, factor_right, vector_parts, inner_parts, image, image_twice, mapped,
+    factor_left, factor_right, vector_parts, inner_parts, image, image_twice, raw, mapped,
     early, late, send_sem, recv_sem,
 ):
     f32, bf16 = jnp.float32, jnp.bfloat16
@@ -449,8 +449,7 @@
         inverse = jnp.where(square > 0.0, lax.rsqrt(square), 0.0)
         return inverse, square * inverse
 
-    inverses, lengths, diagonals = [], [], []
-    for index in range(0, ITERS, 2):
+    def left_stage():
         for power in (0, 1):
             for first in panels:
                 inner = jnp.dot(
@@ -463,40 +462,52 @@
                     rows = slice(first + step, first + step + STRIP)
                     for third, piece in enumerate((high, high, low_part)):
                         inner_parts[power, rows, third * width : (third + 1) * width] = piece
-        if index + 2 == ITERS:
-            b_last.wait_send()
-        crosses = []
-        for power, dest in ((0, image), (1, image_twice)):
-            for first in panels:
-                outer = jnp.dot(
-                    inner_parts[power, first : first + PANEL, :],
-                    factor_right[power],
-                    preferred_element_type=f32,
-                )
-                dest[first : first + PANEL, :] = outer
-                for step in range(0, PANEL, STRIP):
-                    if power == 0:
-                        rows = slice(first + step, first + step + STRIP)
-                        crosses.append(fold(outer[step : step + STRIP] * basis[index, rows, :]))
+
+    def right_stage(power, put):
+        for first in panels:
+            outer = jnp.dot(
+                inner_parts[power, first : first + PANEL, :],
+                factor_right[power],
+                preferred_element_type=f32,
+            )
+            for step in range(0, PANEL, STRIP):
+                put(slice(first + step, first + step + STRIP), outer[step : step + STRIP])
+
+    inverses, lengths, diagonals = [], [], []
+    crosses = []
+
+    def put_image(strip, value):
+        image[strip, :] = value
+        crosses.append(fold(value * basis[0, strip, :]))
+
+    def put_twice(strip, value):
+        image_twice[strip, :] = value
+
+    left_stage()
+    right_stage(0, put_image)
+    right_stage(1, put_twice)
+    for index in range(0, ITERS, 2):
         inverse, length = sized(total(squares))
         diagonal = (total(crosses) * inverse) * inverse
-        ready_now = diagonal == diagonal
-        step_inverse = inverse
         scaled = diagonal * inverse
         ratio = length * inverses[-1] if index > 0 else None
         squares, crosses = [], []
         now, before = (index // 2) % 2, (index // 2 + 1) % 2
         for strip in strips:
-            value = image[strip, :] * step_inverse - scaled * basis[index, strip, :]
+            value = image[strip, :] * inverse - scaled * basis[index, strip, :]
             if index > 0:
                 value = value - ratio * basis[index - 1, strip, :]
             basis[index + 1, strip, :] = value
             squares.append(fold(value * value))
-            beyond = image_twice[strip, :] * step_inverse - scaled * image[strip, :]
+            beyond = image_twice[strip, :] * inverse - scaled * image[strip, :]
             if index > 0:
                 beyond = beyond - ratio * mapped[before, strip, :]
             mapped[now, strip, :] = beyond
             crosses.append(fold(value * beyond))
+            if index + 2 < ITERS:
+                spread_out(strip, beyond)
+        if index + 2 < ITERS:
+            left_stage()
         next_inverse, next_length = sized(total(squares))
         next_diagonal = (total(crosses) * next_inverse) * next_inverse
         inverses += [inverse, next_inverse]
@@ -508,19 +519,37 @@
         if index + 4 == ITERS:
             early[0] = record
             early_copy = spread(early)
+            b_last.wait_send()
         if index + 2 == ITERS:
             late[0] = record
             late_copy = spread(late)
             a_last.wait_send()
         next_scaled, next_ratio = next_diagonal * next_inverse, next_length * inverse
-        squares = []
+        squares, crosses = [], []
         for strip in strips:
             value = (
                 mapped[now, strip, :] * next_inverse - next_ratio * basis[index, strip, :]
             ) - next_scaled * basis[index + 1, strip, :]
             basis[index + 2, strip, :] = value
             if index + 2 < ITERS:
-                squares.append(spread_out(strip, value))
+                squares.append(fold(value * value))
+
+        def next_image(strip, outer):
+            raw[strip, :] = outer
+            value = (
+                outer * next_inverse - next_scaled * mapped[now, strip, :]
+            ) - next_ratio * image[strip, :]
+            image[strip, :] = value
+            crosses.append(fold(value * basis[index + 2, strip, :]))
+
+        def next_twice(strip, outer):
+            image_twice[strip, :] = (
+                outer * next_inverse - next_scaled * raw[strip, :]
+            ) - next_ratio * image_twice[strip, :]
+
+        if index + 2 < ITERS:
+            right_stage(0, next_image)
+            right_stage(1, next_twice)
     inverses.append(jnp.ones((1, 1), f32))
     for copy in sent:
         if copy is not a_last and copy is not b_last:
@@ -723,6 +752,7 @@
             pltpu.VMEM((2, width, 3 * width), bf16),
             pltpu.VMEM((width, width), f32),
             pltpu.VMEM((width, width), f32),
+            pltpu.VMEM((width, width), f32),
             pltpu.VMEM((2, width, width), f32),
             pltpu.VMEM((8 * z_count, 1, 128), f32),
             pltpu.VMEM((8 * z_count, 1, 128), f32),

time: 29.3 us -> 29 us (0.990)
  Pallas kernels: 28.5 us -> 28.2 us
    pallas_call x1, Pallas kernels: 27.5 us -> 27.1 us  [fused_body(): pl.pallas_call(functools.partial(fused_kernel, z_count, 1.0 / (ent_dev *...]
where the time goes in v8:
time: 29 us; the launch traced here: 28.8 us
  Pallas kernels  28.2 us (97%)
  between operations  0.64 us (2%)
    pallas_call x1, Pallas kernels, fused_body(): pl.pallas_call(functools.partial(fused_kernel, z_count, 1.0 / (ent_dev *...  27.1 us
    pallas_call x1, Pallas kernels, fused_body(): pl.pallas_call(finish_kernel, out_shape=(out, out), in_specs=[vmem, vmem,...  1.04 us

profile of v8, /device:TPU:0, one launch (start us, length us, event | category | flops | bytes accessed | tf_op | source)
XLA Modules:
  0.0 28.8 jit_solution(7647776835147973842)
XLA Ops:
  0.6 27.1 %shard_map.59 = (f32[9,256,256]{2,1,0:T(8,128)S(1)}, f32[32,128]{1,0:T(8,128)S(1)}, f32[32,128]{1,0:T(8,128)S(1)}) custom-call(bf16[1024,256]{1,0:T(8,128)(2,1)} %factors_hbm.1, s32[8,1,1,1024]{3,2,1,0:T(1,128)} %heads_hbm.1, s32[8,1,1,1024]{3,2,1,0:T(1,128)} %tails_hbm.1, f32[8,1,1,1024]{3,2,1,0:T(1,128)} %values_hbm.1), custom_call_target="tpu_custom_call" | custom-call | tf_op jit(solution)/shard_map/pallas_call | solution.py:709
  27.8 1.0 %shard_map.60 = (f32[1,256,256]{2,1,0:T(8,128)}, f32[1,256,256]{2,1,0:T(8,128)}) custom-call(f32[9,256,256]{2,1,0:T(8,128)S(1)} %get-tuple-element.5.basis, f32[32,128]{1,0:T(8,128)S(1)} %get-tuple-element.6.mix_ref, f32[32,128]{1,0:T(8,128)S(1)} %get-tuple-element.7.scale_ref), custom_call_target="tpu_custom_call" | custom-call | tf_op jit(solution)/shard_map/pallas_call | solution.py:766

commit v9 on v8

--- a/solution.py
+++ b/solution.py
@@ -115,7 +115,7 @@
 
 
 MESH = pl.DeviceIdType.MESH
-COPIES = 22
+COPIES = 20
 CHUNKS = 4
 STRIP = 32
 PANEL = 128
@@ -177,15 +177,8 @@
     tell(barrier)
     first_q = (1 - e) * 4 + (1 - y) * 2 + 1 - c
     block_count = factors_ref.shape[0]
-    factor_loads = []
-    for block in range(block_count):
-        rows = pl.ds(block * tile_width, tile_width)
-        factor_loads.append(
-            pltpu.make_async_copy(
-                factors_hbm.at[rows], factors_ref.at[block], factor_sem.at[block]
-            )
-        )
-        factor_loads[-1].start()
+    factor_load = pltpu.make_async_copy(factors_hbm, factors_ref, factor_sem)
+    factor_load.start()
     loads = []
     for slot, (source, dest) in enumerate(
         (
@@ -235,8 +228,8 @@
         return copy_to(others, others, pair_peer, pair)
 
     flipped = []
+    factor_load.wait()
     for block in range(block_count):
-        factor_loads[block].wait()
         flipped.append(factors_ref[block].T)
         turned[block] = flipped[-1]
     own_rows = pl.ds(pl.multiple_of(c * half, half), half)
@@ -376,13 +369,14 @@
     gram_line[0] = gram_half[1] + gram_xy[1]
     if z_count > 2:
         pl.semaphore_wait(ready.at[z_count - 3], line_count)
-    line_copies = [
-        send(gram_line.at[0], gram_line.at[z_count - hop], z_peer(hop))
-        for hop in range(1, z_count)
-    ]
+    line_pair = spare()
+    for hop in range(1, z_count):
+        copy_to(gram_line.at[0], gram_line.at[z_count - hop], z_peer(hop), line_pair).start()
+    line_rest = gram_line.at[pl.ds(1, z_count - 1)]
+    line_copy = copy_to(line_rest, line_rest, pair_peer, line_pair)
+    sent.append(line_copy)
     join(3)
-    for copy in line_copies:
-        copy.wait_recv()
+    line_copy.wait_recv()
     for hop in range(z_count):
         place = lax.rem(z + hop, z_count)
         gram_pair[0, pl.ds(pl.multiple_of(place * share, share), share), :] = gram_line[hop]
@@ -726,7 +720,7 @@
             pltpu.SMEM(tails.shape, jnp.int32),
             pltpu.SMEM((1,) + heads.shape[1:], jnp.int32),
             pltpu.SMEM((1,) + heads.shape[1:], jnp.int32),
-            pltpu.SemaphoreType.DMA((ent_dev // tile_width,)),
+            pltpu.SemaphoreType.DMA,
             pltpu.SemaphoreType.DMA((7,)),
             pltpu.SemaphoreType.REGULAR((max(z_count - 2, 1),)),
             pltpu.VMEM((ent_dev // tile_width, width, tile_width), bf16),
@@ -760,7 +754,7 @@
             pltpu.SemaphoreType.DMA((COPIES,)),
         ],
         compiler_params=pltpu.CompilerParams(collective_id=0, has_side_effects=True),
-    )(factors, heads, tails, values)
+    )(factors.reshape(ent_dev // tile_width, tile_width, width), heads, tails, values)
     out = jax.ShapeDtypeStruct((1, width, width), f32)
     anywhere = pl.BlockSpec(memory_space=pl.ANY)
     return pl.pallas_call(

time: 29 us -> 28.7 us (0.990)
  Pallas kernels: 28.2 us -> 27.9 us
where the time goes in v9:
time: 28.7 us; the launch traced here: 28.6 us
  Pallas kernels  27.9 us (97%)
  between operations  0.64 us (2%)
    pallas_call x1, Pallas kernels, fused_body(): pl.pallas_call(functools.partial(fused_kernel, z_count, 1.0 / (ent_dev *...  26.9 us
    pallas_call x1, Pallas kernels, fused_body(): pl.pallas_call(finish_kernel, out_shape=(out, out), in_specs=[vmem, vmem,...  1.04 us

profile of v9, /device:TPU:0, one launch (start us, length us, event | category | flops | bytes accessed | tf_op | source)
XLA Modules:
  0.0 28.6 jit_solution(14628222730903062743)
XLA Ops:
  0.6 26.9 %shard_map.59 = (f32[9,256,256]{2,1,0:T(8,128)S(1)}, f32[32,128]{1,0:T(8,128)S(1)}, f32[32,128]{1,0:T(8,128)S(1)}) custom-call(bf16[8,128,256]{2,1,0:T(8,128)(2,1)} %bitcast.1, s32[8,1,1,1024]{3,2,1,0:T(1,128)} %heads_hbm.1, s32[8,1,1,1024]{3,2,1,0:T(1,128)} %tails_hbm.1, f32[8,1,1,1024]{3,2,1,0:T(1,128)} %values_hbm.1), custom_call_target="tpu_custom_call" | custom-call | tf_op jit(solution)/shard_map/pallas_call | solution.py:703
  27.5 1.0 %shard_map.60 = (f32[1,256,256]{2,1,0:T(8,128)}, f32[1,256,256]{2,1,0:T(8,128)}) custom-call(f32[9,256,256]{2,1,0:T(8,128)S(1)} %get-tuple-element.5.basis, f32[32,128]{1,0:T(8,128)S(1)} %get-tuple-element.6.mix_ref, f32[32,128]{1,0:T(8,128)S(1)} %get-tuple-element.7.scale_ref), custom_call_target="tpu_custom_call" | custom-call | tf_op jit(solution)/shard_map/pallas_call | solution.py:760

commit v10 on v9

--- a/solution.py
+++ b/solution.py
@@ -402,15 +402,19 @@
     panels = range(0, width, PANEL)
     gram = gram_full[...]
     gram_high, gram_low = split(gram)
-    gram_twice = jnp.dot(gram_high, gram_high, preferred_element_type=f32) + (
-        jnp.dot(gram_high, gram_low, preferred_element_type=f32)
-        + jnp.dot(gram_low, gram_high, preferred_element_type=f32)
-    )
-    for power, (high, low_part) in enumerate(((gram_high, gram_low), split(gram_twice))):
+    for third in range(3):
+        span = slice(third * width, (third + 1) * width)
+        factor_left[0, :, span] = (gram_high, gram_low, gram_high)[third]
+        factor_right[0, span, :] = (gram_high, gram_low, gram_high)[third]
+        vector_parts[span, :] = (gram_high, gram_high, gram_low)[third]
+    for first in panels:
+        rows = slice(first, first + PANEL)
+        high, low_part = split(
+            jnp.dot(factor_left[0, rows, :], vector_parts[...], preferred_element_type=f32)
+        )
         for third, piece in enumerate((high, low_part, high)):
-            span = slice(third * width, (third + 1) * width)
-            factor_left[power, :, span] = piece
-            factor_right[power, span, :] = piece
+            factor_left[1, rows, third * width : (third + 1) * width] = piece
+            factor_right[1, third * width + first : third * width + first + PANEL, :] = piece
 
     def spread_out(strip, value):
         high, low_part = split(value)

time: 28.7 us -> 28.6 us (level)
  no operation moved by 1% of the time
where the time goes in v10:
time: 28.6 us; the launch traced here: 28.5 us
  Pallas kernels  27.8 us (97%)
  between operations  0.64 us (2%)
    pallas_call x1, Pallas kernels, fused_body(): pl.pallas_call(functools.partial(fused_kernel, z_count, 1.0 / (ent_dev *...  26.8 us
    pallas_call x1, Pallas kernels, fused_body(): pl.pallas_call(finish_kernel, out_shape=(out, out), in_specs=[vmem, vmem,...  1.04 us

profile of v10, /device:TPU:0, one launch (start us, length us, event | category | flops | bytes accessed | tf_op | source)
XLA Modules:
  0.0 28.5 jit_solution(3379531394903072146)
XLA Ops:
  0.6 26.8 %shard_map.59 = (f32[9,256,256]{2,1,0:T(8,128)S(1)}, f32[32,128]{1,0:T(8,128)S(1)}, f32[32,128]{1,0:T(8,128)S(1)}) custom-call(bf16[8,128,256]{2,1,0:T(8,128)(2,1)} %bitcast.1, s32[8,1,1,1024]{3,2,1,0:T(1,128)} %heads_hbm.1, s32[8,1,1,1024]{3,2,1,0:T(1,128)} %tails_hbm.1, f32[8,1,1,1024]{3,2,1,0:T(1,128)} %values_hbm.1), custom_call_target="tpu_custom_call" | custom-call | tf_op jit(solution)/shard_map/pallas_call | solution.py:707
  27.4 1.0 %shard_map.60 = (f32[1,256,256]{2,1,0:T(8,128)}, f32[1,256,256]{2,1,0:T(8,128)}) custom-call(f32[9,256,256]{2,1,0:T(8,128)S(1)} %get-tuple-element.5.basis, f32[32,128]{1,0:T(8,128)S(1)} %get-tuple-element.6.mix_ref, f32[32,128]{1,0:T(8,128)S(1)} %get-tuple-element.7.scale_ref), custom_call_target="tpu_custom_call" | custom-call | tf_op jit(solution)/shard_map/pallas_call | solution.py:764
